TPU v7x, 32 devices: a whole 2x2x4 slice. The times are simulated.
32 devices in a mesh: dap: 16 (over z, y, x), dp: 2 (over core).
Axes of the slice: x: 2, y: 2, z: 4, core: 2. Of those that a mesh axis runs over, the one named last changes fastest.
Arguments:
- edge_embedding: bfloat16 [192, 96, 128], P(('dp', 'dap')), parts along dimension 0, may hold values from -6 to 6
- alignment_embedding: bfloat16 [128, 96, 256], P('dp', 'dap'), parts along dimension 0, may hold values from -6 to 6
- tensor_flank_matrix: bfloat16 [256, 64], replicated, may hold values from -0.375 to 0.375
- tensor_final_matrix: bfloat16 [1024, 128], replicated, may hold values from -0.75 to 0.75
- outward_sigmoid_matrix: bfloat16 [128, 640], replicated, may hold values from -0.5 to 0.5
- outward_final_matrix: bfloat16 [128, 128], replicated, may hold values from -0.5 to 0.5
- inward_sigmoid_matrix: bfloat16 [128, 640], replicated, may hold values from -0.5 to 0.5
- inward_final_matrix: bfloat16 [128, 128], replicated, may hold values from -0.5 to 0.5
- adjoint_seed: bfloat16 [192, 96, 128], P(('dp', 'dap')), parts along dimension 0, may hold values from -6 to 6
Outputs:
- edge_embedding_updated: bfloat16 [192, 96, 128], P(('dp', 'dap')), parts along dimension 0
- edge_embedding_adjoint: bfloat16 [192, 96, 128], P(('dp', 'dap')), parts along dimension 0
- alignment_adjoint: bfloat16 [128, 96, 256], P('dp', 'dap'), parts along dimension 0
- outer_proj_grad: float32 [512, 64], P('dp'), parts along dimension 0
- outer_final_grad: float32 [2048, 128], P('dp'), parts along dimension 0
- outgoing_proj_grad: float32 [256, 640], P('dp'), parts along dimension 0
- outgoing_final_grad: float32 [256, 128], P('dp'), parts along dimension 0
- incoming_proj_grad: float32 [256, 640], P('dp'), parts along dimension 0
- incoming_final_grad: float32 [256, 128], P('dp'), parts along dimension 0
There are 2 independent parts, one for each index of `dp`. A program takes and returns all parts, laid end to end along the dimension named above; an argument that names none is the same for every part. Nothing has to cross between parts.
All inputs are finite; a program needn't handle non-finite values.
Results may differ from a plain program's by a relative error of at most 0.02.
Values may be sent and summed in bfloat16 or wider, within the bound.
No kernel may reach another device: no remote copies, remote signals or barrier semaphores. Data moves between devices by JAX's collectives and lax.ppermute only.
A program may use at most 128 MiB of HBM per device.

v0:
```python
import jax
import jax.numpy as jnp
from jax import lax
from jax.sharding import PartitionSpec as P

EPSILON = 1e-05


def truncated_numbers(values):
    return lax.optimization_barrier(values.astype(jnp.bfloat16))


def edge_standardized(values, which_axis):
    average = jnp.mean(values, axis=which_axis, keepdims=True)
    centred = values - average
    factor = lax.rsqrt(jnp.mean(centred * centred, axis=which_axis, keepdims=True) + EPSILON)
    return centred * factor


def standardizer_adjoint(values, gradient, which_axis):
    average = jnp.mean(values, axis=which_axis, keepdims=True)
    centred = values - average
    factor = lax.rsqrt(jnp.mean(centred * centred, axis=which_axis, keepdims=True) + EPSILON)
    hatted = centred * factor
    return factor * (
        gradient
        - jnp.mean(gradient, axis=which_axis, keepdims=True)
        - hatted * jnp.mean(gradient * hatted, axis=which_axis, keepdims=True)
    )


def sigmoid_pieces(edge_entry, linear_mapping, latent_tensor):
    standardized_edges = truncated_numbers(edge_standardized(edge_entry.astype(jnp.float32), 2))
    gate_pre = jnp.dot(
        standardized_edges,
        linear_mapping[:, 4 * latent_tensor :],
        preferred_element_type=jnp.float32,
    )
    split_pre = jnp.einsum(
        "rnz,zc->crn",
        standardized_edges,
        linear_mapping[:, : 4 * latent_tensor],
        preferred_element_type=jnp.float32,
    )
    source_masked = truncated_numbers(
        jax.nn.sigmoid(split_pre[:latent_tensor]) * split_pre[latent_tensor : 2 * latent_tensor]
    )
    target_masked = truncated_numbers(
        jax.nn.sigmoid(split_pre[2 * latent_tensor : 3 * latent_tensor])
        * split_pre[3 * latent_tensor :]
    )
    return (standardized_edges, gate_pre, split_pre, source_masked, target_masked)


def grouped(values, groups):
    return values.reshape((groups, values.shape[0] // groups) + values.shape[1:])


def contract_items(left_cols, right_cols, outgoing):
    if outgoing:
        return jnp.einsum(
            "xqik,xqjk->xqij", left_cols, right_cols, preferred_element_type=jnp.float32
        )
    return jnp.einsum("xqki,xqkj->xqij", left_cols, right_cols, preferred_element_type=jnp.float32)


def contract_back_items(grad_cols, left_cols, right_cols, outgoing):
    if outgoing:
        source_adjoint = jnp.einsum(
            "xqij,xqjk->xqik", grad_cols, right_cols, preferred_element_type=jnp.float32
        )
        target_adjoint = jnp.einsum(
            "xqij,xqik->xqjk", grad_cols, left_cols, preferred_element_type=jnp.float32
        )
    else:
        source_adjoint = jnp.einsum(
            "xqij,xqkj->xqki", grad_cols, right_cols, preferred_element_type=jnp.float32
        )
        target_adjoint = jnp.einsum(
            "xqij,xqki->xqkj", grad_cols, left_cols, preferred_element_type=jnp.float32
        )
    return (truncated_numbers(source_adjoint), truncated_numbers(target_adjoint))


def triangle_forward(edge_entry, linear_mapping, final, outgoing):
    latent_tensor = final.shape[0]
    groups = lax.axis_size("dap")
    standardized_edges, gate_pre, split_pre, source_masked, target_masked = sigmoid_pieces(
        edge_entry, linear_mapping, latent_tensor
    )
    triangle_cols = truncated_numbers(
        contract_items(
            lax.all_to_all(
                grouped(source_masked, groups), "dap", split_axis=0, concat_axis=2, tiled=True
            ),
            lax.all_to_all(
                grouped(target_masked, groups), "dap", split_axis=0, concat_axis=2, tiled=True
            ),
            outgoing,
        )
    )
    returned = lax.all_to_all(triangle_cols, "dap", split_axis=2, concat_axis=0, tiled=True)
    result = returned
    returned = result
    triangle = returned.reshape((latent_tensor,) + returned.shape[2:])
    unit_norm = truncated_numbers(edge_standardized(triangle.astype(jnp.float32), 0))
    values = jnp.einsum("crn,cz->rnz", unit_norm, final, preferred_element_type=jnp.float32)
    pair_new = truncated_numbers(edge_entry.astype(jnp.float32) + jax.nn.sigmoid(gate_pre) * values)
    return (pair_new, triangle, None)


def triangle_back(edge_entry, linear_mapping, final, outgoing, triangle, gradient):
    latent_tensor = final.shape[0]
    groups = lax.axis_size("dap")
    standardized_edges, gate_pre, split_pre, source_masked, target_masked = sigmoid_pieces(
        edge_entry, linear_mapping, latent_tensor
    )
    sigmoid_factor = jax.nn.sigmoid(gate_pre)
    tri_wide = triangle.astype(jnp.float32)
    unit_norm = truncated_numbers(edge_standardized(tri_wide, 0))
    values = jnp.einsum("crn,cz->rnz", unit_norm, final, preferred_element_type=jnp.float32)
    scaled = truncated_numbers(gradient * sigmoid_factor)
    final_sum = jnp.einsum("crn,rnz->cz", unit_norm, scaled, preferred_element_type=jnp.float32)
    grad_unit = jnp.einsum("rnz,cz->crn", scaled, final, preferred_element_type=jnp.float32)
    adjoint_sigmoid = truncated_numbers(gradient * values * sigmoid_factor * (1.0 - sigmoid_factor))
    grad_triangle = truncated_numbers(standardizer_adjoint(tri_wide, grad_unit, 0))
    left_back, right_back = contract_back_items(
        lax.all_to_all(
            grouped(grad_triangle, groups), "dap", split_axis=0, concat_axis=2, tiled=True
        ),
        lax.all_to_all(
            grouped(source_masked, groups), "dap", split_axis=0, concat_axis=2, tiled=True
        ),
        lax.all_to_all(
            grouped(target_masked, groups), "dap", split_axis=0, concat_axis=2, tiled=True
        ),
        outgoing,
    )
    source_adjoint = (
        lax.all_to_all(left_back, "dap", split_axis=2, concat_axis=0, tiled=True)
        .reshape(source_masked.shape)
        .astype(jnp.float32)
    )
    target_adjoint = (
        lax.all_to_all(right_back, "dap", split_axis=2, concat_axis=0, tiled=True)
        .reshape(target_masked.shape)
        .astype(jnp.float32)
    )
    logistic_primary = jax.nn.sigmoid(split_pre[:latent_tensor])
    logistic_tertiary = jax.nn.sigmoid(split_pre[2 * latent_tensor : 3 * latent_tensor])
    grad_split = truncated_numbers(
        jnp.concatenate(
            [
                source_adjoint
                * split_pre[latent_tensor : 2 * latent_tensor]
                * logistic_primary
                * (1.0 - logistic_primary),
                source_adjoint * logistic_primary,
                target_adjoint
                * split_pre[3 * latent_tensor :]
                * logistic_tertiary
                * (1.0 - logistic_tertiary),
                target_adjoint * logistic_tertiary,
            ],
            axis=0,
        )
    )
    proj_sum = jnp.concatenate(
        [
            jnp.einsum(
                "rnz,crn->zc", standardized_edges, grad_split, preferred_element_type=jnp.float32
            ),
            jnp.einsum(
                "rnz,rnc->zc",
                standardized_edges,
                adjoint_sigmoid,
                preferred_element_type=jnp.float32,
            ),
        ],
        axis=1,
    )
    grad_norm = jnp.einsum(
        "crn,zc->rnz",
        grad_split,
        linear_mapping[:, : 4 * latent_tensor],
        preferred_element_type=jnp.float32,
    )
    grad_norm = grad_norm + jnp.dot(
        adjoint_sigmoid,
        linear_mapping[:, 4 * latent_tensor :].T,
        preferred_element_type=jnp.float32,
    )
    grad_pair = gradient + standardizer_adjoint(edge_entry.astype(jnp.float32), grad_norm, 2)
    return (grad_pair, proj_sum, final_sum)


def shards(
    edge_embedding,
    alignment_embedding,
    tensor_flank_matrix,
    tensor_final_matrix,
    outward_sigmoid_matrix,
    outward_final_matrix,
    inward_sigmoid_matrix,
    inward_final_matrix,
    adjoint_seed,
):
    rows_here = edge_embedding.shape[0]
    residues = edge_embedding.shape[1]
    alignment_depth = alignment_embedding.shape[0]
    contraction_extent = tensor_flank_matrix.shape[1] // 2
    alignment_standardized = truncated_numbers(
        edge_standardized(alignment_embedding.astype(jnp.float32), 2)
    )
    alignment_mapped = jnp.dot(
        alignment_standardized, tensor_flank_matrix, preferred_element_type=jnp.float32
    )
    tensor_source_factor = truncated_numbers(alignment_mapped[..., :contraction_extent])
    tensor_target_factor = truncated_numbers(alignment_mapped[..., contraction_extent:])
    right_all = lax.all_gather(
        tensor_target_factor.reshape(alignment_depth, rows_here * contraction_extent),
        "dap",
        axis=1,
        tiled=True,
    )
    right_all = right_all.reshape(alignment_depth, residues, contraction_extent)
    tile_lines = 128 if residues % 128 == 0 else residues
    tile_number = residues // tile_lines
    outer_parts = []
    first_parts = []
    for block_index in range(tile_number):
        lower = block_index * tile_lines
        right_block = right_all[:, lower : lower + tile_lines]
        triangle_contraction = jnp.einsum(
            "sic,sjd->ijcd", tensor_source_factor, right_block, preferred_element_type=jnp.float32
        )
        outer_block = truncated_numbers(
            triangle_contraction.reshape(
                rows_here, tile_lines, contraction_extent * contraction_extent
            )
            / alignment_depth
        )
        update = jnp.dot(outer_block, tensor_final_matrix, preferred_element_type=jnp.float32)
        first_parts.append(
            truncated_numbers(
                edge_embedding[:, lower : lower + tile_lines].astype(jnp.float32) + update
            )
        )
        outer_parts.append(outer_block)
    outer_mean = jnp.concatenate(outer_parts, axis=1)
    pair_one = jnp.concatenate(first_parts, axis=1)
    pair_two, triangle_out, kept_out = triangle_forward(
        pair_one, outward_sigmoid_matrix, outward_final_matrix, True
    )
    edge_embedding_updated, triangle_in, kept_in = triangle_forward(
        pair_two, inward_sigmoid_matrix, inward_final_matrix, False
    )
    grad_two, inward_sigmoid_accrual, inward_final_accrual = triangle_back(
        pair_two,
        inward_sigmoid_matrix,
        inward_final_matrix,
        False,
        triangle_in,
        adjoint_seed.astype(jnp.float32),
    )
    grad_one, outward_sigmoid_accrual, outward_final_accrual = triangle_back(
        pair_one, outward_sigmoid_matrix, outward_final_matrix, True, triangle_out, grad_two
    )
    edge_embedding_adjoint = truncated_numbers(grad_one)
    tensor_final_accrual = jnp.einsum(
        "rnk,rnz->kz", outer_mean, edge_embedding_adjoint, preferred_element_type=jnp.float32
    )
    source_adjoint = jnp.zeros((alignment_depth, rows_here, contraction_extent), jnp.float32)
    outer_grads = []
    for block_index in range(tile_number):
        lower = block_index * tile_lines
        right_block = right_all[:, lower : lower + tile_lines]
        adjoint_tensor_mean = truncated_numbers(
            jnp.dot(
                edge_embedding_adjoint[:, lower : lower + tile_lines],
                tensor_final_matrix.T,
                preferred_element_type=jnp.float32,
            )
        )
        adjoint_tensor_mean = adjoint_tensor_mean.reshape(
            rows_here, tile_lines, contraction_extent, contraction_extent
        )
        source_adjoint = (
            source_adjoint
            + jnp.einsum(
                "mopz,loz->lmp",
                adjoint_tensor_mean,
                right_block,
                preferred_element_type=jnp.float32,
            )
            / alignment_depth
        )
        outer_grads.append(adjoint_tensor_mean)
    pair_columns = lax.all_to_all(
        edge_embedding_adjoint, "dap", split_axis=1, concat_axis=0, tiled=True
    )
    left_all = lax.all_gather(
        tensor_source_factor.reshape(alignment_depth, rows_here * contraction_extent),
        "dap",
        axis=1,
        tiled=True,
    )
    left_all = left_all.reshape(alignment_depth, residues, contraction_extent)
    target_adjoint = jnp.zeros((alignment_depth, rows_here, contraction_extent), jnp.float32)
    for block_index in range(tile_number):
        lower = block_index * tile_lines
        column_grad = truncated_numbers(
            jnp.dot(
                pair_columns[lower : lower + tile_lines],
                tensor_final_matrix.T,
                preferred_element_type=jnp.float32,
            )
        )
        column_grad = column_grad.reshape(
            tile_lines, rows_here, contraction_extent, contraction_extent
        )
        target_adjoint = (
            target_adjoint
            + jnp.einsum(
                "gxqp,vgq->vxp",
                column_grad,
                left_all[:, lower : lower + tile_lines],
                preferred_element_type=jnp.float32,
            )
            / alignment_depth
        )
    alignment_mapped_adjoint = truncated_numbers(
        jnp.concatenate([source_adjoint, target_adjoint], axis=2)
    )
    tensor_flank_accrual = jnp.einsum(
        "ajo,ajm->om",
        alignment_standardized,
        alignment_mapped_adjoint,
        preferred_element_type=jnp.float32,
    )
    alignment_standard_adjoint = jnp.dot(
        alignment_mapped_adjoint, tensor_flank_matrix.T, preferred_element_type=jnp.float32
    )
    alignment_adjoint = truncated_numbers(
        standardizer_adjoint(alignment_embedding.astype(jnp.float32), alignment_standard_adjoint, 2)
    )
    totals = lax.psum(
        (
            tensor_flank_accrual,
            tensor_final_accrual,
            outward_sigmoid_accrual,
            outward_final_accrual,
            inward_sigmoid_accrual,
            inward_final_accrual,
        ),
        "dap",
    )
    return (
        edge_embedding_updated,
        edge_embedding_adjoint,
        alignment_adjoint,
        totals[0] / residues,
        totals[1] / residues,
        totals[2] / residues,
        totals[3] / residues,
        totals[4] / residues,
        totals[5] / residues,
    )


def solution(mesh):
    placed = (
        P(("dp", "dap"), None, None),
        P("dp", "dap", None),
        P(),
        P(),
        P(),
        P(),
        P(),
        P(),
        P(("dp", "dap"), None, None),
    )
    return jax.shard_map(
        shards,
        mesh=mesh,
        in_specs=placed,
        out_specs=(
            P(("dp", "dap"), None, None),
            P(("dp", "dap"), None, None),
            P("dp", "dap", None),
            P("dp", None),
            P("dp", None),
            P("dp", None),
            P("dp", None),
            P("dp", None),
            P("dp", None),
        ),
        check_vma=False,
    )
```

profile of v0, /device:TPU:0, one launch (start us, length us, event | category | flops | bytes accessed | tf_op | source)
XLA Modules:
  0.0 465.5 jit_solution(12668008011917967780)
XLA Ops:
  12.3 45.3 %all-gather = bf16[16,192,64]{1,2,0:T(8,128)(2,1)S(1)} all-gather(bf16[1,192,64]{1,2,0:T(8,128)(2,1)S(1)} %bitcast.310), channel_id=1, replica_groups=mesh['dap'=16,'dp'=2] {'dap'}, dimensions={0}, use_global_device_ids=true | all-gather | bytes 417792 | tf_op jit(solution)/shard_map/all_gather | solution.py:220
  67.4 3.5 all-to-all-start.1
  72.7 6.3 %all-to-all-done.1 = bf16[16,8,6,96]{3,1,2,0:T(8,128)(2,1)S(1)} async-done(((bf16[16,8,6,96]{3,1,2,0:T(8,128)(2,1)}), bf16[16,8,6,96]{3,1,2,0:T(8,128)(2,1)S(1)}, u32[]{:S(2)}, u32[]{:S(2)}) %all-to-all-start.1) | async-done | bytes 147488 | tf_op jit(solution)/shard_map/all_to_all | solution.py:96
  79.0 14.1 %all_to_all.182 = bf16[16,8,6,96]{3,1,2,0:T(8,128)(2,1)S(1)} all-to-all(bf16[16,8,6,96]{3,1,2,0:T(8,128)(2,1)S(1)} %copy.173), channel_id=1, replica_groups=mesh['dap'=16,'dp'=2] {'dap'}, dimensions={0} | all-to-all | bytes 294912 | tf_op jit(solution)/shard_map/all_to_all | solution.py:93
  93.4 11.3 %all_to_all.183 = bf16[1,8,96,96]{3,1,0,2:T(8,128)(2,1)S(1)} all-to-all(bf16[1,8,96,96]{3,1,0,2:T(8,128)(2,1)S(1)} %copy.178), channel_id=1, replica_groups=mesh['dap'=16,'dp'=2] {'dap'}, dimensions={2} | all-to-all | bytes 294912 | tf_op jit(solution)/shard_map/all_to_all | solution.py:102
  117.2 4.2 all-to-all-start.3
  124.8 4.7 %all-to-all-done.3 = bf16[16,8,6,96]{3,1,2,0:T(8,128)(2,1)} async-done(((bf16[16,8,6,96]{3,1,2,0:T(8,128)(2,1)}), bf16[16,8,6,96]{3,1,2,0:T(8,128)(2,1)}, u32[]{:S(2)}, u32[]{:S(2)}) %all-to-all-start.3) | async-done | bytes 147488 | tf_op jit(solution)/shard_map/all_to_all | solution.py:93
  129.5 11.6 %all_to_all.184 = bf16[16,8,6,96]{3,1,2,0:T(8,128)(2,1)S(1)} all-to-all(bf16[16,8,6,96]{3,1,2,0:T(8,128)(2,1)} %copy.185), channel_id=1, replica_groups=mesh['dap'=16,'dp'=2] {'dap'}, dimensions={0} | all-to-all | bytes 294912 | tf_op jit(solution)/shard_map/all_to_all | solution.py:96
  142.4 11.1 %all_to_all.185 = bf16[1,8,96,96]{3,1,0,2:T(8,128)(2,1)S(1)} all-to-all(bf16[1,8,96,96]{3,1,0,2:T(8,128)(2,1)S(1)} %copy.188), channel_id=1, replica_groups=mesh['dap'=16,'dp'=2] {'dap'}, dimensions={2} | all-to-all | bytes 294912 | tf_op jit(solution)/shard_map/all_to_all | solution.py:102
  166.3 4.2 all-to-all-start.6
  170.6 8.0 %all-to-all-done.6 = bf16[16,8,6,96]{3,1,2,0:T(8,128)(2,1)} async-done(((bf16[16,8,6,96]{3,1,2,0:T(8,128)(2,1)}), bf16[16,8,6,96]{3,1,2,0:T(8,128)(2,1)}, u32[]{:S(2)}, u32[]{:S(2)}) %all-to-all-start.6) | async-done | bytes 147488 | tf_op jit(solution)/shard_map/all_to_all | solution.py:128
  180.6 4.2 all-to-all-start.7
  184.8 44.5 %all-gather.1 = bf16[16,192,64]{1,2,0:T(8,128)(2,1)S(1)} all-gather(bf16[1,192,64]{1,2,0:T(8,128)(2,1)S(1)} %bitcast.309), channel_id=1, replica_groups=mesh['dap'=16,'dp'=2] {'dap'}, dimensions={0}, use_global_device_ids=true | all-gather | bytes 417792 | tf_op jit(solution)/shard_map/all_gather | solution.py:302
  242.3 4.2 all-to-all-start.8
  251.9 3.7 all-to-all-done.8
  268.5 4.2 all-to-all-start.9
  278.2 3.3 all-to-all-done.9
  285.3 4.2 all-to-all-start.10
  293.5 4.1 all-to-all-done.10
  297.6 3.5 all-to-all-start.11
  306.4 2.7 all-to-all-done.11
  320.0 4.2 all-to-all-start.12
  327.8 4.5 all-to-all-done.12
  338.7 113.7 %all-reduce.3.cloned.1.call-done = (f32[256,64]{0,1:T(8,128)}, f32[1024,128]{1,0:T(8,128)}, f32[128,640]{1,0:T(8,128)}, f32[128,128]{1,0:T(8,128)}, f32[128,640]{1,0:T(8,128)}, /*index=5*/f32[128,128]{1,0:T(8,128)}) async-done(((f32[256,64]{0,1:T(8,128)}, f32[1024,128]{1,0:T(8,128)}, f32[128,640]{1,0:T(8,128)}, f32[128,128]{1,0:T(8,128)}, f32[128,640]{1,0:T(8,128)}, /*index=5*/f32[128,128]{1,0:T(8,128)}), ...) | async-done | bytes 1376272 | tf_op jit(solution)/shard_map/psum | solution.py:347
  (256 shorter events, 125.4 us)
Async XLA Ops:
  7.2 54.5 %copy-start = (bf16[1024,128]{1,0:T(8,128)(2,1)S(1)}, bf16[1024,128]{1,0:T(8,128)(2,1)}, u32[]{:S(2)}) copy-start(bf16[1024,128]{1,0:T(8,128)(2,1)} %param.12) | copy-start | bytes 786436
  12.2 46.7 %copy-start.37 = (bf16[64,6,32]{0,2,1:T(8,128)(2,1)}, bf16[64,6,32]{0,2,1:T(8,128)(2,1)S(1)}, u32[]{:S(2)}) copy-start(bf16[64,6,32]{0,2,1:T(8,128)(2,1)S(1)} %get-tuple-element.46) | copy-start | bytes 73732
  67.4 11.6 %all-to-all-start.1 = ((bf16[16,8,6,96]{3,1,2,0:T(8,128)(2,1)}), bf16[16,8,6,96]{3,1,2,0:T(8,128)(2,1)S(1)}, u32[]{:S(2)}, u32[]{:S(2)}) async-start(bf16[16,8,6,96]{3,1,2,0:T(8,128)(2,1)} %copy.175), calls=%async_computation.1 | async-start | bytes 393216 | tf_op jit(solution)/shard_map/all_to_all | solution.py:96
  79.0 26.5 %copy-start.20 = (bf16[16,8,6,96]{3,1,2,0:T(8,128)(2,1)}, bf16[16,8,6,96]{3,1,2,0:T(8,128)(2,1)S(1)}, u32[]{:S(2)}) copy-start(bf16[16,8,6,96]{3,1,2,0:T(8,128)(2,1)S(1)} %all-to-all-done.1) | copy-start | bytes 442372
  93.0 12.4 %copy-start.21 = (bf16[16,8,6,96]{3,1,2,0:T(8,128)(2,1)}, bf16[16,8,6,96]{3,1,2,0:T(8,128)(2,1)S(1)}, u32[]{:S(2)}) copy-start(bf16[16,8,6,96]{3,1,2,0:T(8,128)(2,1)S(1)} %all_to_all.182) | copy-start | bytes 442372
  93.4 14.6 %copy-start.46 = (bf16[128,128]{1,0:T(8,128)(2,1)S(1)}, bf16[128,128]{1,0:T(8,128)(2,1)}, u32[]{:S(2)}) copy-start(bf16[128,128]{1,0:T(8,128)(2,1)} %param.14) | copy-start | bytes 98308
  117.2 12.3 %all-to-all-start.3 = ((bf16[16,8,6,96]{3,1,2,0:T(8,128)(2,1)}), bf16[16,8,6,96]{3,1,2,0:T(8,128)(2,1)}, u32[]{:S(2)}, u32[]{:S(2)}) async-start(bf16[16,8,6,96]{3,1,2,0:T(8,128)(2,1)} %copy.183), calls=%async_computation.3 | async-start | bytes 393216 | tf_op jit(solution)/shard_map/all_to_all | solution.py:93
  142.4 16.0 %copy-start.45 = (bf16[128,128]{1,0:T(8,128)(2,1)S(1)}, bf16[128,128]{1,0:T(8,128)(2,1)}, u32[]{:S(2)}) copy-start(bf16[128,128]{1,0:T(8,128)(2,1)} %param.16) | copy-start | bytes 98308
  161.4 9.1 %copy-start.38 = (bf16[64,6,32]{0,2,1:T(8,128)(2,1)S(1)}, bf16[64,6,32]{0,2,1:T(8,128)(2,1)}, u32[]{:S(2)}) copy-start(bf16[64,6,32]{0,2,1:T(8,128)(2,1)} %copy-done.37) | copy-start | bytes 73732
  166.3 12.3 %all-to-all-start.6 = ((bf16[16,8,6,96]{3,1,2,0:T(8,128)(2,1)}), bf16[16,8,6,96]{3,1,2,0:T(8,128)(2,1)}, u32[]{:S(2)}, u32[]{:S(2)}) async-start(bf16[16,8,6,96]{3,1,2,0:T(8,128)(2,1)} %copy.193), calls=%async_computation.6 | async-start | bytes 393216 | tf_op jit(solution)/shard_map/all_to_all | solution.py:128
  180.6 61.7 %all-to-all-start.7 = ((bf16[1,8,96,96]{3,1,0,2:T(8,128)(2,1)}), bf16[1,8,96,96]{3,1,0,2:T(8,128)(2,1)}, u32[]{:S(2)}, u32[]{:S(2)}) async-start(bf16[1,8,96,96]{3,1,0,2:T(8,128)(2,1)} %copy.196), calls=%async_computation.7 | async-start | bytes 393216 | tf_op jit(solution)/shard_map/all_to_all | solution.py:140
  242.3 13.3 %all-to-all-start.8 = ((bf16[1,8,96,96]{3,1,0,2:T(8,128)(2,1)}), bf16[1,8,96,96]{3,1,0,2:T(8,128)(2,1)}, u32[]{:S(2)}, u32[]{:S(2)}) async-start(bf16[1,8,96,96]{3,1,0,2:T(8,128)(2,1)} %copy.203), calls=%async_computation.8 | async-start | bytes 393216 | tf_op jit(solution)/shard_map/all_to_all | solution.py:145
  266.7 9.8 %copy-start.15 = (bf16[6,96,128]{2,1,0:T(8,128)(2,1)S(1)}, bf16[6,96,128]{2,1,0:T(8,128)(2,1)}, u32[]{:S(2)}) copy-start(bf16[6,96,128]{2,1,0:T(8,128)(2,1)} %copy-done.14) | copy-start | bytes 442372
  268.5 13.0 %all-to-all-start.9 = ((bf16[16,8,6,96]{3,1,2,0:T(8,128)(2,1)}), bf16[16,8,6,96]{3,1,2,0:T(8,128)(2,1)}, u32[]{:S(2)}, u32[]{:S(2)}) async-start(bf16[16,8,6,96]{3,1,2,0:T(8,128)(2,1)} %copy.209), calls=%async_computation.9 | async-start | bytes 393216 | tf_op jit(solution)/shard_map/all_to_all | solution.py:128
  274.5 14.9 %copy-start.17 = (bf16[6,96,128]{2,1,0:T(8,128)(2,1)S(1)}, bf16[6,96,128]{2,1,0:T(8,128)(2,1)}, u32[]{:S(2)}) copy-start(bf16[6,96,128]{2,1,0:T(8,128)(2,1)} %copy-done.16) | copy-start | bytes 442372
  285.3 12.3 %all-to-all-start.10 = ((bf16[1,8,96,96]{3,1,0,2:T(8,128)(2,1)}), bf16[1,8,96,96]{3,1,0,2:T(8,128)(2,1)}, u32[]{:S(2)}, u32[]{:S(2)}) async-start(bf16[1,8,96,96]{3,1,0,2:T(8,128)(2,1)} %copy.212), calls=%async_computation.10 | async-start | bytes 393216 | tf_op jit(solution)/shard_map/all_to_all | solution.py:140
  297.6 11.6 %all-to-all-start.11 = ((bf16[1,8,96,96]{3,1,0,2:T(8,128)(2,1)}), bf16[1,8,96,96]{3,1,0,2:T(8,128)(2,1)S(1)}, u32[]{:S(2)}, u32[]{:S(2)}) async-start(bf16[1,8,96,96]{3,1,0,2:T(8,128)(2,1)} %copy.219), calls=%async_computation.11 | async-start | bytes 393216 | tf_op jit(solution)/shard_map/all_to_all | solution.py:145
  315.4 3.6 copy-start.13
  319.0 5.5 %copy-start.6 = (bf16[6,96,1024]{2,1,0:T(8,128)(2,1)S(1)}, bf16[6,96,1024]{2,1,0:T(8,128)(2,1)}, u32[]{:S(2)}) copy-start(bf16[6,96,1024]{2,1,0:T(8,128)(2,1)} %convolution_convert_fusion.1) | copy-start | bytes 3538948
  320.0 12.3 %all-to-all-start.12 = ((bf16[6,96,128]{2,0,1:T(8,128)(2,1)}), bf16[6,96,128]{2,0,1:T(8,128)(2,1)}, u32[]{:S(2)}, u32[]{:S(2)}) async-start(bf16[6,96,128]{2,0,1:T(8,128)(2,1)} %copy.230), calls=%async_computation.12 | async-start | bytes 393216 | tf_op jit(solution)/shard_map/all_to_all | solution.py:299
  324.2 128.2 %all-reduce.3.cloned.1.call-start = ((), (), s32[]{:S(2)}) async-start(), calls=%async_computation.13 | async-start | bytes 2752512 | tf_op jit(solution)/shard_map/psum | solution.py:347
  452.4 4.2 copy-start.57
  452.4 4.9 %copy-start.39 = (f32[128,640]{1,0:T(8,128)S(1)}, f32[128,640]{1,0:T(8,128)}, u32[]{:S(2)}) copy-start(f32[128,640]{1,0:T(8,128)} %get-tuple-element.23) | copy-start | bytes 983044
  454.0 4.1 copy-start.56
  (44 other events, 59.1 us)
Sparse Core Ops, SparseCore 0:
  337.5 114.9 all-reduce.2
where the time goes:
time: 468 us; the launch traced here: 466 us
  waiting for transfers between devices  151 us (32%)
  blocking collectives  138 us (29%)
  local copies, waits for them, and re-layouts  56.8 us (12%)
  starting transfers between devices  36.5 us (8%)
  matrix products  34.6 us (7%)
  other arithmetic  33.8 us (7%)
  between operations  15.1 us (3%)
    psum x1, waiting for transfers between devices, shards(): lax.psum((tensor_flank_accrual, tensor_final_accrual, outward_sigmoid_acc...  114 us
    all_gather x1, blocking collectives, shards(): lax.all_gather(tensor_target_factor.reshape(alignment_depth, rows_here *...  45.3 us
    all_gather x1, blocking collectives, shards(): lax.all_gather(tensor_source_factor.reshape(alignment_depth, rows_here *...  44.5 us
    all_to_all x2, blocking collectives, triangle_forward(): lax.all_to_all(triangle_cols, 'dap', split_axis=2, concat_axis=0, tiled=T...  22.3 us
    unnamed x120, local copies, waits for them, and re-layouts  14.3 us
    all_to_all x1, blocking collectives, triangle_forward(): lax.all_to_all(grouped(source_masked, groups), 'dap', split_axis=0, conca...  14.1 us
    optimization_barrier x15, local copies, waits for them, and re-layouts, truncated_numbers(): return lax.optimization_barrier(values.astype(jnp.bfloat16))  13.9 us
    all_to_all x1, blocking collectives, triangle_forward(): lax.all_to_all(grouped(target_masked, groups), 'dap', split_axis=0, conca...  11.6 us
  transfers between devices with their start and end apart: 10, of which 9 were waited for; matrix products, arithmetic and copies ran while one was open for 9% of the time, Pallas kernels for 0%

commit v1 on v0

--- a/solution.py
+++ b/solution.py
@@ -56,6 +56,60 @@
     return values.reshape((groups, values.shape[0] // groups) + values.shape[1:])
 
 
+def gathered(values, axis):
+    groups = lax.axis_size("dap")
+    copies = jnp.broadcast_to(values[None], (groups,) + values.shape)
+    return jnp.moveaxis(lax.all_to_all(copies, "dap", 0, 0, tiled=True), 0, axis)
+
+
+def exchanged(values):
+    return lax.all_to_all(values, "dap", split_axis=0, concat_axis=0, tiled=True)
+
+
+def totalled(parts):
+    groups = lax.axis_size("dap")
+    flat = jnp.concatenate([part.reshape(-1) for part in parts])
+    unit = groups * 16 * 128
+    padded = -(-flat.size // unit) * unit
+    blocks = jnp.pad(flat, (0, padded - flat.size)).reshape(groups, -1, 128)
+    mine = exchanged(truncated_numbers(blocks)).astype(jnp.float32).sum(axis=0)
+    whole = gathered(truncated_numbers(mine), 0).astype(jnp.float32).reshape(-1)
+    out, place = [], 0
+    for part in parts:
+        out.append(whole[place : place + part.size].reshape(part.shape))
+        place += part.size
+    return out
+
+
+def to_channels(*rows):
+    groups = lax.axis_size("dap")
+    packed = jnp.stack([grouped(values, groups) for values in rows], axis=1)
+    received = exchanged(packed)
+    return [
+        jnp.moveaxis(received[:, at], 0, 1).reshape(
+            received.shape[2], -1, received.shape[4]
+        )[None]
+        for at in range(len(rows))
+    ]
+
+
+def to_rows(*columns):
+    groups = lax.axis_size("dap")
+    packed = jnp.stack(
+        [
+            jnp.moveaxis(
+                values[0].reshape(values.shape[1], groups, -1, values.shape[3]), 1, 0
+            )
+            for values in columns
+        ],
+        axis=1,
+    )
+    received = exchanged(packed)
+    return [
+        received[:, at].reshape((-1,) + received.shape[3:]) for at in range(len(columns))
+    ]
+
+
 def contract_items(left_cols, right_cols, outgoing):
     if outgoing:
         return jnp.einsum(
@@ -88,28 +142,16 @@
     standardized_edges, gate_pre, split_pre, source_masked, target_masked = sigmoid_pieces(
         edge_entry, linear_mapping, latent_tensor
     )
-    triangle_cols = truncated_numbers(
-        contract_items(
-            lax.all_to_all(
-                grouped(source_masked, groups), "dap", split_axis=0, concat_axis=2, tiled=True
-            ),
-            lax.all_to_all(
-                grouped(target_masked, groups), "dap", split_axis=0, concat_axis=2, tiled=True
-            ),
-            outgoing,
-        )
-    )
-    returned = lax.all_to_all(triangle_cols, "dap", split_axis=2, concat_axis=0, tiled=True)
-    result = returned
-    returned = result
-    triangle = returned.reshape((latent_tensor,) + returned.shape[2:])
+    kept = to_channels(source_masked, target_masked)
+    triangle_cols = truncated_numbers(contract_items(kept[0], kept[1], outgoing))
+    (triangle,) = to_rows(triangle_cols)
     unit_norm = truncated_numbers(edge_standardized(triangle.astype(jnp.float32), 0))
     values = jnp.einsum("crn,cz->rnz", unit_norm, final, preferred_element_type=jnp.float32)
     pair_new = truncated_numbers(edge_entry.astype(jnp.float32) + jax.nn.sigmoid(gate_pre) * values)
-    return (pair_new, triangle, None)
-
-
-def triangle_back(edge_entry, linear_mapping, final, outgoing, triangle, gradient):
+    return (pair_new, triangle, kept)
+
+
+def triangle_back(edge_entry, linear_mapping, final, outgoing, triangle, kept, gradient):
     latent_tensor = final.shape[0]
     groups = lax.axis_size("dap")
     standardized_edges, gate_pre, split_pre, source_masked, target_masked = sigmoid_pieces(
@@ -124,28 +166,11 @@
     grad_unit = jnp.einsum("rnz,cz->crn", scaled, final, preferred_element_type=jnp.float32)
     adjoint_sigmoid = truncated_numbers(gradient * values * sigmoid_factor * (1.0 - sigmoid_factor))
     grad_triangle = truncated_numbers(standardizer_adjoint(tri_wide, grad_unit, 0))
-    left_back, right_back = contract_back_items(
-        lax.all_to_all(
-            grouped(grad_triangle, groups), "dap", split_axis=0, concat_axis=2, tiled=True
-        ),
-        lax.all_to_all(
-            grouped(source_masked, groups), "dap", split_axis=0, concat_axis=2, tiled=True
-        ),
-        lax.all_to_all(
-            grouped(target_masked, groups), "dap", split_axis=0, concat_axis=2, tiled=True
-        ),
-        outgoing,
-    )
-    source_adjoint = (
-        lax.all_to_all(left_back, "dap", split_axis=2, concat_axis=0, tiled=True)
-        .reshape(source_masked.shape)
-        .astype(jnp.float32)
-    )
-    target_adjoint = (
-        lax.all_to_all(right_back, "dap", split_axis=2, concat_axis=0, tiled=True)
-        .reshape(target_masked.shape)
-        .astype(jnp.float32)
-    )
+    (gradient_cols,) = to_channels(grad_triangle)
+    left_back, right_back = contract_back_items(gradient_cols, kept[0], kept[1], outgoing)
+    source_adjoint, target_adjoint = [
+        values.astype(jnp.float32) for values in to_rows(left_back, right_back)
+    ]
     logistic_primary = jax.nn.sigmoid(split_pre[:latent_tensor])
     logistic_tertiary = jax.nn.sigmoid(split_pre[2 * latent_tensor : 3 * latent_tensor])
     grad_split = truncated_numbers(
@@ -217,13 +242,9 @@
     )
     tensor_source_factor = truncated_numbers(alignment_mapped[..., :contraction_extent])
     tensor_target_factor = truncated_numbers(alignment_mapped[..., contraction_extent:])
-    right_all = lax.all_gather(
-        tensor_target_factor.reshape(alignment_depth, rows_here * contraction_extent),
-        "dap",
-        axis=1,
-        tiled=True,
-    )
-    right_all = right_all.reshape(alignment_depth, residues, contraction_extent)
+    right_all = gathered(tensor_target_factor, 1).reshape(
+        alignment_depth, residues, contraction_extent
+    )
     tile_lines = 128 if residues % 128 == 0 else residues
     tile_number = residues // tile_lines
     outer_parts = []
@@ -261,10 +282,11 @@
         inward_final_matrix,
         False,
         triangle_in,
+        kept_in,
         adjoint_seed.astype(jnp.float32),
     )
     grad_one, outward_sigmoid_accrual, outward_final_accrual = triangle_back(
-        pair_one, outward_sigmoid_matrix, outward_final_matrix, True, triangle_out, grad_two
+        pair_one, outward_sigmoid_matrix, outward_final_matrix, True, triangle_out, kept_out, grad_two
     )
     edge_embedding_adjoint = truncated_numbers(grad_one)
     tensor_final_accrual = jnp.einsum(
@@ -299,13 +321,9 @@
     pair_columns = lax.all_to_all(
         edge_embedding_adjoint, "dap", split_axis=1, concat_axis=0, tiled=True
     )
-    left_all = lax.all_gather(
-        tensor_source_factor.reshape(alignment_depth, rows_here * contraction_extent),
-        "dap",
-        axis=1,
-        tiled=True,
-    )
-    left_all = left_all.reshape(alignment_depth, residues, contraction_extent)
+    left_all = gathered(tensor_source_factor, 1).reshape(
+        alignment_depth, residues, contraction_extent
+    )
     target_adjoint = jnp.zeros((alignment_depth, rows_here, contraction_extent), jnp.float32)
     for block_index in range(tile_number):
         lower = block_index * tile_lines
@@ -344,7 +362,7 @@
     alignment_adjoint = truncated_numbers(
         standardizer_adjoint(alignment_embedding.astype(jnp.float32), alignment_standard_adjoint, 2)
     )
-    totals = lax.psum(
+    totals = totalled(
         (
             tensor_flank_accrual,
             tensor_final_accrual,
@@ -352,8 +370,7 @@
             outward_final_accrual,
             inward_sigmoid_accrual,
             inward_final_accrual,
-        ),
-        "dap",
+        )
     )
     return (
         edge_embedding_updated,

time: 468 us -> 257 us (0.55)
  waiting for transfers between devices: 151 us -> 39.7 us
  blocking collectives: 138 us -> 80.6 us
  between operations: 15.1 us -> 2.19 us
  other arithmetic: 33.8 us -> 21.7 us
  matrix products: 34.6 us -> 22.9 us
  local copies, waits for them, and re-layouts: 56.8 us -> 50.1 us
    psum x1 -> x0, waiting for transfers between devices: 114 us -> none  [shards(): lax.psum((tensor_flank_accrual, tensor_final_accrual, outward_sigmoid_acc...]
    all_gather x2 -> x0, blocking collectives: 89.8 us -> none  [the longest x1 45.3 us: shards(): lax.all_gather(tensor_target_factor.reshape(alignment_depth, rows_here *...]
    all_to_all x4 -> x6, blocking collectives: 47.9 us -> 80.6 us  [exchanged(): lax.all_to_all(values, 'dap', split_axis=0, concat_axis=0, tiled=True)]
    reshape x10 -> x5, local copies, waits for them, and re-layouts: 12.9 us -> 6.04 us  [the longest x1 2.73 us: shards(): gathered(tensor_source_factor, 1)]
    all_to_all x8 -> x6, waiting for transfers between devices: 32.8 us -> 36.6 us  [the longest x3 23.9 us: gathered(): lax.all_to_all(copies, 'dap', 0, 0, tiled=True)]
    all_to_all x8 -> x6, starting transfers between devices: 32.1 us -> 34.1 us  [the longest x3 17.9 us: exchanged(): lax.all_to_all(values, 'dap', split_axis=0, concat_axis=0, tiled=True)]
    unnamed x120 -> x156, local copies, waits for them, and re-layouts: 14.3 us -> 15.8 us
  transfers between devices with their start and end apart: 10 -> 7, of which waited for: 9 -> 6; matrix products, arithmetic and copies ran while one was open for 9% -> 13% of each run, Pallas kernels for 0% -> 0%
where the time goes in v1:
time: 257 us; the launch traced here: 255 us
  blocking collectives  80.6 us (31%)
  local copies, waits for them, and re-layouts  50.1 us (19%)
  waiting for transfers between devices  39.7 us (15%)
  starting transfers between devices  37.9 us (15%)
  matrix products  22.9 us (9%)
  other arithmetic  21.7 us (8%)
    all_to_all x6, blocking collectives, exchanged(): lax.all_to_all(values, 'dap', split_axis=0, concat_axis=0, tiled=True)  80.6 us
    all_to_all x3, waiting for transfers between devices, gathered(): lax.all_to_all(copies, 'dap', 0, 0, tiled=True)  23.9 us
    all_to_all x3, starting transfers between devices, exchanged(): lax.all_to_all(values, 'dap', split_axis=0, concat_axis=0, tiled=True)  17.9 us
    all_to_all x3, starting transfers between devices, gathered(): lax.all_to_all(copies, 'dap', 0, 0, tiled=True)  16.2 us
    unnamed x156, local copies, waits for them, and re-layouts  15.8 us
    all_to_all x3, waiting for transfers between devices, exchanged(): lax.all_to_all(values, 'dap', split_axis=0, concat_axis=0, tiled=True)  12.8 us
    optimization_barrier x15, local copies, waits for them, and re-layouts, truncated_numbers(): return lax.optimization_barrier(values.astype(jnp.bfloat16))  9.37 us
    convert_element_type x13, other arithmetic, truncated_numbers(): return lax.optimization_barrier(values.astype(jnp.bfloat16))  7.83 us
  transfers between devices with their start and end apart: 7, of which 6 were waited for; matrix products, arithmetic and copies ran while one was open for 13% of the time, Pallas kernels for 0%

profile of v1, /device:TPU:0, one launch (start us, length us, event | category | flops | bytes accessed | tf_op | source)
XLA Modules:
  0.0 255.0 jit_solution(16639720308278416110)
XLA Ops:
  6.6 8.3 %all-to-all-start = ((bf16[16,2,6144]{2,1,0:T(2,128)(2,1)}), bf16[16,2,6144]{2,1,0:T(2,128)(2,1)S(1)}, u32[]{:S(2)}, u32[]{:S(2)}) async-start(bf16[16,2,6144]{2,1,0:T(2,128)(2,1)} %reshape.289), calls=%async_computation | async-start | bytes 786432 | tf_op jit(solution)/shard_map/all_to_all | solution.py:62
  14.9 12.6 %all-to-all-done = bf16[16,2,6144]{2,1,0:T(2,128)(2,1)S(1)} async-done(((bf16[16,2,6144]{2,1,0:T(2,128)(2,1)}), bf16[16,2,6144]{2,1,0:T(2,128)(2,1)S(1)}, u32[]{:S(2)}, u32[]{:S(2)}) %all-to-all-start) | async-done | bytes 393248 | tf_op jit(solution)/shard_map/all_to_all | solution.py:62
  32.4 15.4 %all_to_all.78 = bf16[16,2,8,6,96]{4,2,3,1,0:T(8,128)(2,1)S(1)} all-to-all(bf16[16,2,8,6,96]{4,2,3,1,0:T(8,128)(2,1)S(1)} %copy.175), channel_id=1, replica_groups=mesh['dap'=16,'dp'=2] {'dap'}, dimensions={0} | all-to-all | bytes 589824 | tf_op jit(solution)/shard_map/all_to_all | solution.py:66
  48.5 11.5 %all_to_all.79 = bf16[16,1,8,6,96]{4,2,3,1,0:T(8,128)(2,1)S(1)} all-to-all(bf16[16,1,8,6,96]{4,2,3,1,0:T(8,128)(2,1)S(1)} %bitcast.340), channel_id=1, replica_groups=mesh['dap'=16,'dp'=2] {'dap'}, dimensions={0} | all-to-all | bytes 294912 | tf_op jit(solution)/shard_map/all_to_all | solution.py:66
  71.3 13.2 %all_to_all.80 = bf16[16,2,8,6,96]{4,2,3,1,0:T(8,128)(2,1)S(1)} all-to-all(bf16[16,2,8,6,96]{4,2,3,1,0:T(8,128)(2,1)S(1)} %copy.186), channel_id=1, replica_groups=mesh['dap'=16,'dp'=2] {'dap'}, dimensions={0} | all-to-all | bytes 589824 | tf_op jit(solution)/shard_map/all_to_all | solution.py:66
  85.3 11.8 %all_to_all.81 = bf16[16,1,8,6,96]{4,2,3,1,0:T(8,128)(2,1)S(1)} all-to-all(bf16[16,1,8,6,96]{4,2,3,1,0:T(8,128)(2,1)S(1)} %bitcast.341), channel_id=1, replica_groups=mesh['dap'=16,'dp'=2] {'dap'}, dimensions={0} | all-to-all | bytes 294912 | tf_op jit(solution)/shard_map/all_to_all | solution.py:66
  98.5 1.9 copy.194
  104.6 2.1 fusion.79
  111.1 11.1 %all_to_all.82 = bf16[16,1,8,6,96]{4,2,3,1,0:T(8,128)(2,1)S(1)} all-to-all(bf16[16,1,8,6,96]{4,2,3,1,0:T(8,128)(2,1)S(1)} %copy.196), channel_id=1, replica_groups=mesh['dap'=16,'dp'=2] {'dap'}, dimensions={0} | all-to-all | bytes 294912 | tf_op jit(solution)/shard_map/all_to_all | solution.py:66
  124.7 4.4 %all-to-all-start.6 = ((bf16[16,2,8,6,96]{4,2,3,1,0:T(8,128)(2,1)}), bf16[16,2,8,6,96]{4,2,3,1,0:T(8,128)(2,1)}, u32[]{:S(2)}, u32[]{:S(2)}) async-start(bf16[16,2,8,6,96]{4,2,3,1,0:T(8,128)(2,1)} %copy.203), calls=%async_computation.6 | async-start | bytes 786432 | tf_op jit(solution)/shard_map/all_to_all | solution.py:66
  130.9 2.7 %reshape.291 = bf16[16,2,6144]{2,1,0:T(2,128)(2,1)} reshape(bf16[16,6,32,64]{3,2,1,0:T(8,128)(2,1)} %broadcast_bitcast_fusion) | data formatting | bytes 786432
  133.6 4.9 %all-to-all-done.6 = bf16[16,2,8,6,96]{4,2,3,1,0:T(8,128)(2,1)} async-done(((bf16[16,2,8,6,96]{4,2,3,1,0:T(8,128)(2,1)}), bf16[16,2,8,6,96]{4,2,3,1,0:T(8,128)(2,1)}, u32[]{:S(2)}, u32[]{:S(2)}) %all-to-all-start.6) | async-done | bytes 294944 | tf_op jit(solution)/shard_map/all_to_all | solution.py:66
  138.6 4.2 %all-to-all-start.9 = ((bf16[16,2,6144]{2,1,0:T(2,128)(2,1)}), bf16[16,2,6144]{2,1,0:T(2,128)(2,1)}, u32[]{:S(2)}, u32[]{:S(2)}) async-start(bf16[16,2,6144]{2,1,0:T(2,128)(2,1)} %reshape.291), calls=%async_computation.9 | async-start | bytes 786432 | tf_op jit(solution)/shard_map/all_to_all | solution.py:62
  157.4 6.9 %all-to-all-start.7 = ((bf16[16,1,8,6,96]{4,2,3,1,0:T(8,128)(2,1)}), bf16[16,1,8,6,96]{4,2,3,1,0:T(8,128)(2,1)}, u32[]{:S(2)}, u32[]{:S(2)}) async-start(bf16[16,1,8,6,96]{4,2,3,1,0:T(8,128)(2,1)} %copy.211), calls=%async_computation.7 | async-start | bytes 393216 | tf_op jit(solution)/shard_map/all_to_all | solution.py:66
  164.3 2.7 %reshape.292 = bf16[16,6,32,64]{3,2,1,0:T(8,128)(2,1)} reshape(bf16[16,2,6144]{2,1,0:T(2,128)(2,1)} %all-to-all-done.9) | data formatting | bytes 786432
  167.0 2.7 %copy.232 = bf16[64,96,32]{1,0,2:T(8,128)(2,1)} copy(bf16[64,96,32]{0,2,1:T(8,128)(2,1)} %bitcast.322) | data formatting | bytes 786432 | tf_op jit(solution)/shard_map/reshape | solution.py:324
  176.0 6.7 %all-to-all-start.8 = ((bf16[16,2,8,6,96]{4,2,3,1,0:T(8,128)(2,1)}), bf16[16,2,8,6,96]{4,2,3,1,0:T(8,128)(2,1)S(1)}, u32[]{:S(2)}, u32[]{:S(2)}) async-start(bf16[16,2,8,6,96]{4,2,3,1,0:T(8,128)(2,1)} %copy.218), calls=%async_computation.8 | async-start | bytes 786432 | tf_op jit(solution)/shard_map/all_to_all | solution.py:66
  184.6 7.6 %all-to-all-done.8 = bf16[16,2,8,6,96]{4,2,3,1,0:T(8,128)(2,1)S(1)} async-done(((bf16[16,2,8,6,96]{4,2,3,1,0:T(8,128)(2,1)}), bf16[16,2,8,6,96]{4,2,3,1,0:T(8,128)(2,1)S(1)}, u32[]{:S(2)}, u32[]{:S(2)}) %all-to-all-start.8) | async-done | bytes 294944 | tf_op jit(solution)/shard_map/all_to_all | solution.py:66
  196.4 3.8 %all-to-all-start.10 = ((bf16[6,96,128]{2,0,1:T(8,128)(2,1)}), bf16[6,96,128]{2,0,1:T(8,128)(2,1)S(1)}, u32[]{:S(2)}, u32[]{:S(2)}) async-start(bf16[6,96,128]{2,0,1:T(8,128)(2,1)} %copy.228), calls=%async_computation.10 | async-start | bytes 393216 | tf_op jit(solution)/shard_map/all_to_all | solution.py:321
  202.6 2.6 %fusion.28 = bf16[64,6,32]{0,2,1:T(8,128)(2,1)} fusion(bf16[6,96,32,32]{1,3,2,0:T(8,128)(2,1)} %bitcast.338, bf16[64,96,32]{1,0,2:T(8,128)(2,1)S(1)} %copy-done.46), kind=kOutput, calls=%fused_computation.47 | convolution fusion | flops 75522048 | bytes 1597440 | tf_op jit(solution)/shard_map/mopz,loz->lmp/dot_general | solution.py:312
  205.3 3.0 %all-to-all-done.10 = bf16[6,96,128]{2,0,1:T(8,128)(2,1)S(1)} async-done(((bf16[6,96,128]{2,0,1:T(8,128)(2,1)}), bf16[6,96,128]{2,0,1:T(8,128)(2,1)S(1)}, u32[]{:S(2)}, u32[]{:S(2)}) %all-to-all-start.10) | async-done | bytes 147488 | tf_op jit(solution)/shard_map/all_to_all | solution.py:321
  213.4 17.6 %all_to_all.83 = bf16[16,176,128]{2,1,0:T(8,128)(2,1)S(1)} all-to-all(bf16[16,176,128]{2,1,0:T(8,128)(2,1)S(1)} %bitcast.323), channel_id=1, replica_groups=mesh['dap'=16,'dp'=2] {'dap'}, dimensions={0} | all-to-all | bytes 1441792 | tf_op jit(solution)/shard_map/all_to_all | solution.py:66
  232.1 3.6 %all-to-all-start.12 = ((bf16[16,176,128]{2,1,0:T(8,128)(2,1)}), bf16[16,176,128]{2,1,0:T(8,128)(2,1)S(1)}, u32[]{:S(2)}, u32[]{:S(2)}) async-start(bf16[16,176,128]{2,1,0:T(8,128)(2,1)} %broadcast_in_dim.8), calls=%async_computation.12 | async-start | bytes 1441792 | tf_op jit(solution)/shard_map/all_to_all | solution.py:62
  237.1 11.2 %all-to-all-done.12 = bf16[16,176,128]{2,1,0:T(8,128)(2,1)S(1)} async-done(((bf16[16,176,128]{2,1,0:T(8,128)(2,1)}), bf16[16,176,128]{2,1,0:T(8,128)(2,1)S(1)}, u32[]{:S(2)}, u32[]{:S(2)}) %all-to-all-start.12) | async-done | bytes 720928 | tf_op jit(solution)/shard_map/all_to_all | solution.py:62
  (298 shorter events, 80.2 us)
Async XLA Ops:
  0.6 29.3 %copy-start = (bf16[1024,128]{1,0:T(8,128)(2,1)S(1)}, bf16[1024,128]{1,0:T(8,128)(2,1)}, u32[]{:S(2)}) copy-start(bf16[1024,128]{1,0:T(8,128)(2,1)} %param.12) | copy-start | bytes 786436
  5.1 22.9 %copy-start.47 = (bf16[64,6,32]{0,2,1:T(8,128)(2,1)}, bf16[64,6,32]{0,2,1:T(8,128)(2,1)S(1)}, u32[]{:S(2)}) copy-start(bf16[64,6,32]{0,2,1:T(8,128)(2,1)S(1)} %get-tuple-element.79) | copy-start | bytes 73732
  6.6 21.0 %all-to-all-start = ((bf16[16,2,6144]{2,1,0:T(2,128)(2,1)}), bf16[16,2,6144]{2,1,0:T(2,128)(2,1)S(1)}, u32[]{:S(2)}, u32[]{:S(2)}) async-start(bf16[16,2,6144]{2,1,0:T(2,128)(2,1)} %reshape.289), calls=%async_computation | async-start | bytes 786432 | tf_op jit(solution)/shard_map/all_to_all | solution.py:62
  31.3 30.2 %copy-start.12 = (bf16[6,96,128]{2,1,0:T(8,128)(2,1)}, bf16[6,96,128]{2,1,0:T(8,128)(2,1)S(1)}, u32[]{:S(2)}) copy-start(bf16[6,96,128]{2,1,0:T(8,128)(2,1)S(1)} %fusion.58) | copy-start | bytes 442372
  47.9 12.2 %copy-start.18 = (bf16[16,1,8,6,96]{4,2,3,1,0:T(8,128)(2,1)}, bf16[16,1,8,6,96]{4,2,3,1,0:T(8,128)(2,1)S(1)}, u32[]{:S(2)}) copy-start(bf16[16,1,8,6,96]{4,2,3,1,0:T(8,128)(2,1)S(1)} %get-tuple-element.78) | copy-start | bytes 442372
  48.1 13.2 %copy-start.54 = (bf16[128,128]{1,0:T(8,128)(2,1)S(1)}, bf16[128,128]{1,0:T(8,128)(2,1)}, u32[]{:S(2)}) copy-start(bf16[128,128]{1,0:T(8,128)(2,1)} %param.14) | copy-start | bytes 98308
  110.1 13.3 %copy-start.22 = (bf16[16,1,8,6,96]{4,2,3,1,0:T(8,128)(2,1)S(1)}, bf16[16,1,8,6,96]{4,2,3,1,0:T(8,128)(2,1)}, u32[]{:S(2)}) copy-start(bf16[16,1,8,6,96]{4,2,3,1,0:T(8,128)(2,1)} %copy-done.21) | copy-start | bytes 442372
  124.7 13.9 %all-to-all-start.6 = ((bf16[16,2,8,6,96]{4,2,3,1,0:T(8,128)(2,1)}), bf16[16,2,8,6,96]{4,2,3,1,0:T(8,128)(2,1)}, u32[]{:S(2)}, u32[]{:S(2)}) async-start(bf16[16,2,8,6,96]{4,2,3,1,0:T(8,128)(2,1)} %copy.203), calls=%async_computation.6 | async-start | bytes 786432 | tf_op jit(solution)/shard_map/all_to_all | solution.py:66
  138.6 18.8 %all-to-all-start.9 = ((bf16[16,2,6144]{2,1,0:T(2,128)(2,1)}), bf16[16,2,6144]{2,1,0:T(2,128)(2,1)}, u32[]{:S(2)}, u32[]{:S(2)}) async-start(bf16[16,2,6144]{2,1,0:T(2,128)(2,1)} %reshape.291), calls=%async_computation.9 | async-start | bytes 786432 | tf_op jit(solution)/shard_map/all_to_all | solution.py:62
  155.6 11.4 %copy-start.31 = (bf16[6,96,128]{2,1,0:T(8,128)(2,1)}, bf16[6,96,128]{2,1,0:T(8,128)(2,1)S(1)}, u32[]{:S(2)}) copy-start(bf16[6,96,128]{2,1,0:T(8,128)(2,1)S(1)} %multiply_convert_fusion.7) | copy-start | bytes 442372
  157.4 15.0 %all-to-all-start.7 = ((bf16[16,1,8,6,96]{4,2,3,1,0:T(8,128)(2,1)}), bf16[16,1,8,6,96]{4,2,3,1,0:T(8,128)(2,1)}, u32[]{:S(2)}, u32[]{:S(2)}) async-start(bf16[16,1,8,6,96]{4,2,3,1,0:T(8,128)(2,1)} %copy.211), calls=%async_computation.7 | async-start | bytes 393216 | tf_op jit(solution)/shard_map/all_to_all | solution.py:66
  167.0 4.4 %copy-start.15 = (bf16[6,96,128]{2,1,0:T(8,128)(2,1)S(1)}, bf16[6,96,128]{2,1,0:T(8,128)(2,1)}, u32[]{:S(2)}) copy-start(bf16[6,96,128]{2,1,0:T(8,128)(2,1)} %copy-done.14) | copy-start | bytes 442372
  167.0 4.4 %copy-start.39 = (bf16[6,96,128]{2,1,0:T(8,128)(2,1)S(1)}, bf16[6,96,128]{2,1,0:T(8,128)(2,1)}, u32[]{:S(2)}) copy-start(bf16[6,96,128]{2,1,0:T(8,128)(2,1)} %get-tuple-element.68) | copy-start | bytes 442372
  169.7 4.9 %copy-start.19 = (bf16[16,1,8,6,96]{4,2,3,1,0:T(8,128)(2,1)S(1)}, bf16[16,1,8,6,96]{4,2,3,1,0:T(8,128)(2,1)}, u32[]{:S(2)}) copy-start(bf16[16,1,8,6,96]{4,2,3,1,0:T(8,128)(2,1)} %copy-done.18) | copy-start | bytes 442372
  175.1 7.9 %copy-start.52 = (bf16[128,128]{1,0:T(8,128)(2,1)S(1)}, bf16[128,128]{1,0:T(8,128)(2,1)}, u32[]{:S(2)}) copy-start(bf16[128,128]{1,0:T(8,128)(2,1)} %fusion.36) | copy-start | bytes 98308
  175.2 8.6 %copy-start.13 = (bf16[6,96,128]{2,1,0:T(8,128)(2,1)S(1)}, bf16[6,96,128]{2,1,0:T(8,128)(2,1)}, u32[]{:S(2)}) copy-start(bf16[6,96,128]{2,1,0:T(8,128)(2,1)} %copy-done.12) | copy-start | bytes 442372
  175.2 8.6 %copy-start.24 = (bf16[6,96,128]{2,1,0:T(8,128)(2,1)S(1)}, bf16[6,96,128]{2,1,0:T(8,128)(2,1)}, u32[]{:S(2)}) copy-start(bf16[6,96,128]{2,1,0:T(8,128)(2,1)} %get-tuple-element.46) | copy-start | bytes 442372
  176.0 16.3 %all-to-all-start.8 = ((bf16[16,2,8,6,96]{4,2,3,1,0:T(8,128)(2,1)}), bf16[16,2,8,6,96]{4,2,3,1,0:T(8,128)(2,1)S(1)}, u32[]{:S(2)}, u32[]{:S(2)}) async-start(bf16[16,2,8,6,96]{4,2,3,1,0:T(8,128)(2,1)} %copy.218), calls=%async_computation.8 | async-start | bytes 786432 | tf_op jit(solution)/shard_map/all_to_all | solution.py:66
  196.4 11.9 %all-to-all-start.10 = ((bf16[6,96,128]{2,0,1:T(8,128)(2,1)}), bf16[6,96,128]{2,0,1:T(8,128)(2,1)S(1)}, u32[]{:S(2)}, u32[]{:S(2)}) async-start(bf16[6,96,128]{2,0,1:T(8,128)(2,1)} %copy.228), calls=%async_computation.10 | async-start | bytes 393216 | tf_op jit(solution)/shard_map/all_to_all | solution.py:321
  231.0 4.7 %copy-start.3 = (bf16[64,6,256]{2,0,1:T(8,128)(2,1)S(1)}, bf16[64,6,256]{2,0,1:T(8,128)(2,1)}, u32[]{:S(2)}) copy-start(bf16[64,6,256]{2,0,1:T(8,128)(2,1)} %param.10) | copy-start | bytes 589828
  231.0 4.7 %copy-start.50 = (bf16[256,64]{0,1:T(8,128)(2,1)S(1)}, bf16[256,64]{0,1:T(8,128)(2,1)}, u32[]{:S(2)}) copy-start(bf16[256,64]{0,1:T(8,128)(2,1)} %param.11) | copy-start | bytes 98308
  231.0 4.7 %copy-start.57 = (f32[64,6]{0,1:T(8,128)S(1)}, f32[64,6]{0,1:T(8,128)}, u32[]{:S(2)}) copy-start(f32[64,6]{0,1:T(8,128)} %copy-done.56) | copy-start | bytes 4612
  231.0 4.7 %copy-start.65 = (f32[64,6]{0,1:T(8,128)S(1)}, f32[64,6]{0,1:T(8,128)}, u32[]{:S(2)}) copy-start(f32[64,6]{0,1:T(8,128)} %copy-done.64) | copy-start | bytes 4612
  232.1 16.2 %all-to-all-start.12 = ((bf16[16,176,128]{2,1,0:T(8,128)(2,1)}), bf16[16,176,128]{2,1,0:T(8,128)(2,1)S(1)}, u32[]{:S(2)}, u32[]{:S(2)}) async-start(bf16[16,176,128]{2,1,0:T(8,128)(2,1)} %broadcast_in_dim.8), calls=%async_computation.12 | async-start | bytes 1441792 | tf_op jit(solution)/shard_map/all_to_all | solution.py:62
  (56 other events, 91.6 us)

commit v2 on v1

--- a/solution.py
+++ b/solution.py
@@ -1,6 +1,10 @@
+from functools import partial
+
 import jax
 import jax.numpy as jnp
 from jax import lax
+from jax.experimental import pallas as pl
+from jax.experimental.pallas import tpu as pltpu
 from jax.sharding import PartitionSpec as P
 
 EPSILON = 1e-05
@@ -385,6 +389,753 @@
     )
 
 
+F32 = jnp.float32
+BF16 = jnp.bfloat16
+LANES = 128
+SUB = 8
+
+
+def nn(a, b):
+    return lax.dot_general(a, b, (((1,), (0,)), ((), ())), preferred_element_type=F32)
+
+
+def nt(a, b):
+    return lax.dot_general(a, b, (((1,), (1,)), ((), ())), preferred_element_type=F32)
+
+
+def tn(a, b):
+    return lax.dot_general(a, b, (((0,), (0,)), ((), ())), preferred_element_type=F32)
+
+
+def launch(body, outs, args, scratch=(), name=None, flops=2e8):
+    vmem = pl.BlockSpec(memory_space=pltpu.VMEM)
+    moved = sum(a.size * a.dtype.itemsize for a in args) + sum(
+        o.size * o.dtype.itemsize for o in outs
+    )
+    return pl.pallas_call(
+        body,
+        out_shape=outs,
+        in_specs=[vmem] * len(args),
+        out_specs=[vmem] * len(outs),
+        scratch_shapes=list(scratch),
+        name=name,
+        cost_estimate=pl.CostEstimate(
+            flops=int(flops), bytes_accessed=int(moved), transcendentals=0
+        ),
+        compiler_params=pltpu.CompilerParams(vmem_limit_bytes=40 * 1024 * 1024),
+    )(*args)
+
+
+def moments(x, axis):
+    average = jnp.mean(x, axis=axis, keepdims=True)
+    centred = x - average
+    factor = lax.rsqrt(jnp.mean(centred * centred, axis=axis, keepdims=True) + EPSILON)
+    return centred * factor, factor
+
+
+def moments_adjoint(hatted, factor, gradient, axis):
+    return factor * (
+        gradient
+        - jnp.mean(gradient, axis=axis, keepdims=True)
+        - hatted * jnp.mean(gradient * hatted, axis=axis, keepdims=True)
+    )
+
+
+def tall(x):
+    return jnp.concatenate([x, jnp.zeros((LANES - x.shape[0], x.shape[1]), x.dtype)], axis=0)
+
+
+def dealt(x, groups):
+    return x.reshape((groups, x.shape[0] // groups) + x.shape[1:])
+
+
+def gated_pair(projected, width):
+    left = jax.nn.sigmoid(projected[:width]) * projected[width : 2 * width]
+    right = jax.nn.sigmoid(projected[2 * width : 3 * width]) * projected[3 * width : 4 * width]
+    return left, right
+
+
+def send_pair(out_ref, row, left, right, groups):
+    both = jnp.concatenate([dealt(left, groups), dealt(right, groups)], axis=1)
+    wide = both.shape[1]
+    out_ref[:, row * wide : (row + 1) * wide, :] = both.astype(BF16)
+
+
+def msa_kernel(sizes, msa_ref, flank_t_ref, send_ref, normal_ref, left_ref):
+    rows, depth, hidden, groups = sizes
+    for row in range(rows):
+        hatted, _ = moments(msa_ref[row].astype(F32), 1)
+        normal = hatted.astype(BF16)
+        normal_ref[row] = normal
+        twice = jnp.concatenate([normal, normal], axis=0)
+        mapped = nt(flank_t_ref[...], twice)
+        lane = lax.broadcasted_iota(jnp.int32, (hidden, LANES), 1)
+        low = lane < depth
+        left = mapped[:hidden]
+        left_ref[row * hidden : (row + 1) * hidden] = jnp.where(low, left, 0.0).astype(BF16)
+        left_ref[(rows + row) * hidden : (rows + row + 1) * hidden] = jnp.where(
+            low, 0.0, left
+        ).astype(BF16)
+        half = hidden // 2
+        right = jnp.where(
+            low[:half], mapped[hidden : hidden + half], mapped[hidden + half :]
+        ).astype(BF16)
+        for group in range(groups):
+            send_ref[group, row * half : (row + 1) * half, :] = right
+
+
+def outer_kernel(
+    sizes,
+    right_ref,
+    left_ref,
+    edge_ref,
+    final_t_ref,
+    gates_t_ref,
+    send_ref,
+    spread_ref,
+    outer_ref,
+    pair_ref,
+    wide_ref,
+):
+    rows, residues, depth, hidden, groups, width = sizes
+    half = hidden // 2
+    wide_ref[...] = right_ref[...].reshape(wide_ref.shape).astype(F32)
+    for d in range(half):
+        picked = wide_ref[pl.ds(d, residues, stride=half), :]
+        spread_ref[d * LANES : (d + 1) * LANES, :] = tall(picked).astype(BF16)
+    for d in range(0, half, 2):
+        block = nt(left_ref[...], spread_ref[d * LANES : (d + 2) * LANES, :]) / depth
+        for e in range(2):
+            for h in range(2):
+                for row in range(rows):
+                    at = (h * rows + row) * hidden
+                    to = (h * half + d + e) * hidden
+                    outer_ref[to : to + hidden, row * LANES : (row + 1) * LANES] = block[
+                        at : at + hidden, e * LANES : (e + 1) * LANES
+                    ].astype(BF16)
+    update = nn(final_t_ref[...], outer_ref[...])
+    for row in range(rows):
+        lanes = slice(row * LANES, (row + 1) * LANES)
+        entry = tall(edge_ref[row].astype(F32)).T
+        pair = (entry + update[:, lanes]).astype(BF16)
+        pair_ref[:, lanes] = pair
+        hatted, _ = moments(pair.astype(F32), 0)
+        projected = nn(gates_t_ref[: 4 * width, :], hatted.astype(BF16))
+        left, right = gated_pair(projected, width)
+        send_pair(send_ref, row, left, right, groups)
+
+
+def triangle_kernel(sizes, outgoing, both_ref, send_ref, wide_ref, result_ref):
+    residues, share = sizes
+    wide_ref[...] = both_ref[...].reshape(wide_ref.shape).astype(F32)
+    for c in range(share):
+        left = wide_ref[pl.ds(c, residues, stride=2 * share), :].astype(BF16)
+        right = wide_ref[pl.ds(share + c, residues, stride=2 * share), :].astype(BF16)
+        if outgoing:
+            product = nt(left, tall(right))
+        else:
+            product = tn(left, right)[:residues]
+        result_ref[pl.ds(c, residues, stride=share), :] = product
+    send_ref[...] = result_ref[...].astype(BF16).reshape(send_ref.shape)
+
+
+def triangle_adjoint_kernel(
+    sizes, outgoing, both_ref, grad_ref, send_ref, wide_ref, tri_ref, result_ref
+):
+    residues, share, rows, riders = sizes
+    own = rows * share
+    wide_ref[...] = both_ref[...].reshape(wide_ref.shape).astype(F32)
+    tri_ref[...] = grad_ref[:, :own, :].astype(F32).reshape(tri_ref.shape)
+    for c in range(share):
+        left = wide_ref[pl.ds(c, residues, stride=2 * share), :].astype(BF16)
+        right = wide_ref[pl.ds(share + c, residues, stride=2 * share), :].astype(BF16)
+        grad = tri_ref[pl.ds(c, residues, stride=share), :].astype(BF16)
+        if outgoing:
+            grad_left = nn(grad, tall(right))
+            grad_right = tn(grad, left)[:residues]
+        else:
+            grad_left = nt(right, tall(grad))
+            grad_right = nn(left, tall(grad))
+        result_ref[pl.ds(c, residues, stride=2 * share), :] = grad_left
+        result_ref[pl.ds(share + c, residues, stride=2 * share), :] = grad_right
+    groups = send_ref.shape[0]
+    send_ref[:, : 2 * own, :] = (
+        result_ref[...].astype(BF16).reshape(groups, 2 * own, LANES)
+    )
+    if riders:
+        summed = jnp.sum(grad_ref[:, own:, :].astype(F32), axis=0).astype(BF16)
+        for group in range(groups):
+            send_ref[group, 2 * own :, :] = summed
+
+
+def middle_kernel(
+    sizes,
+    tri_ref,
+    pair_ref,
+    gates_t_ref,
+    final_t_ref,
+    next_gates_t_ref,
+    send_ref,
+    next_ref,
+):
+    rows, groups, width = sizes
+    share = width // groups
+    received = tri_ref[...].astype(F32)
+    for row in range(rows):
+        lanes = slice(row * LANES, (row + 1) * LANES)
+        tri = received[:, row * share : (row + 1) * share, :].reshape(width, LANES)
+        unit, _ = moments(tri, 0)
+        values = nn(final_t_ref[...], unit.astype(BF16))
+        pair = pair_ref[:, lanes].astype(F32)
+        hatted, _ = moments(pair, 0)
+        gate = jax.nn.sigmoid(nn(gates_t_ref[4 * width :, :], hatted.astype(BF16)))
+        following = (pair + gate * values).astype(BF16)
+        next_ref[:, lanes] = following
+        hatted, _ = moments(following.astype(F32), 0)
+        projected = nn(next_gates_t_ref[: 4 * width, :], hatted.astype(BF16))
+        left, right = gated_pair(projected, width)
+        send_pair(send_ref, row, left, right, groups)
+
+
+def tri_adjoint_row(tri, pair, gradient, gates_t_ref, final_ref, final_t_ref, width):
+    hatted_tri, factor = moments(tri, 0)
+    unit = hatted_tri.astype(BF16)
+    values = nn(final_t_ref[...], unit)
+    hatted, _ = moments(pair, 0)
+    gate = jax.nn.sigmoid(nn(gates_t_ref[4 * width :, :], hatted.astype(BF16)))
+    scaled = (gradient * gate).astype(BF16)
+    grad_unit = nn(final_ref[...], scaled)
+    grad_tri = moments_adjoint(hatted_tri, factor, grad_unit, 0)
+    grad_gate = (gradient * values * gate * (1.0 - gate)).astype(BF16)
+    return unit, scaled, values, gate, grad_tri, grad_gate
+
+
+def turn_kernel(
+    sizes,
+    tri_ref,
+    pair_ref,
+    seed_ref,
+    gates_t_ref,
+    final_ref,
+    final_t_ref,
+    send_ref,
+    out_ref,
+    seed_t_ref,
+    grad_gate_ref,
+    final_sum_ref,
+    grads_ref,
+    unit_ref,
+    scaled_ref,
+):
+    rows, residues, groups, width = sizes
+    share = width // groups
+    received = tri_ref[...].astype(F32)
+    for row in range(rows):
+        lanes = slice(row * LANES, (row + 1) * LANES)
+        tri = received[:, row * share : (row + 1) * share, :].reshape(width, LANES)
+        pair = pair_ref[:, lanes].astype(F32)
+        gradient = tall(seed_ref[row].astype(F32)).T
+        seed_t_ref[:, lanes] = gradient.astype(BF16)
+        unit, scaled, values, gate, grad_tri, grad_gate = tri_adjoint_row(
+            tri, pair, gradient, gates_t_ref, final_ref, final_t_ref, width
+        )
+        unit_ref[:, lanes] = unit
+        scaled_ref[:, lanes] = scaled
+        grad_gate_ref[:, lanes] = grad_gate
+        grads_ref[:, row * share : (row + 1) * share, :] = dealt(grad_tri, groups)
+        out_ref[row] = (pair + gate * values).T[:residues].astype(BF16)
+    send_ref[...] = grads_ref[...].astype(BF16)
+    final_sum_ref[...] = nt(unit_ref[...], scaled_ref[...])
+
+
+def proj_adjoint_row(row, received, pair, grad_gate, gates_t_ref, gates_ref, normal_ref, proj_ref, width):
+    share2 = received.shape[1]
+    lanes = slice(row * LANES, (row + 1) * LANES)
+    grad_left = received[:, : share2 // 2, :].reshape(width, LANES)
+    grad_right = received[:, share2 // 2 :, :].reshape(width, LANES)
+    hatted, factor = moments(pair, 0)
+    normal = hatted.astype(BF16)
+    normal_ref[:, lanes] = normal
+    projected = nn(gates_t_ref[: 4 * width, :], normal)
+    first = jax.nn.sigmoid(projected[:width])
+    third = jax.nn.sigmoid(projected[2 * width : 3 * width])
+    left_part = grad_left * first
+    right_part = grad_right * third
+    proj_ref[:width, lanes] = (
+        left_part * projected[width : 2 * width] * (1.0 - first)
+    ).astype(BF16)
+    proj_ref[width : 2 * width, lanes] = left_part.astype(BF16)
+    proj_ref[2 * width : 3 * width, lanes] = (
+        right_part * projected[3 * width :] * (1.0 - third)
+    ).astype(BF16)
+    proj_ref[3 * width : 4 * width, lanes] = right_part.astype(BF16)
+    proj_ref[4 * width :, lanes] = grad_gate
+    grad_normal = nn(gates_ref[...], proj_ref[:, lanes])
+    return moments_adjoint(hatted, factor, grad_normal, 0)
+
+
+def deal_rows(out_ref, start, total, groups):
+    for tile in range(total.shape[1] // LANES):
+        block = dealt(total[:, tile * LANES : (tile + 1) * LANES], groups)
+        out_ref[:, start : start + block.shape[1], :] = block
+        start += block.shape[1]
+    return start
+
+
+def between_kernel(
+    sizes,
+    both_ref,
+    pair_in_ref,
+    seed_ref,
+    grad_gate_in_ref,
+    gates_in_t_ref,
+    gates_in_ref,
+    final_in_sum_ref,
+    tri_ref,
+    pair_out_ref,
+    gates_out_t_ref,
+    final_out_ref,
+    final_out_t_ref,
+    send_ref,
+    grad_ref,
+    grad_gate_ref,
+    grads_ref,
+    normal_ref,
+    proj_ref,
+    unit_ref,
+    scaled_ref,
+):
+    rows, groups, width = sizes
+    share = width // groups
+    received = tri_ref[...].astype(F32)
+    for row in range(rows):
+        lanes = slice(row * LANES, (row + 1) * LANES)
+        pair = pair_in_ref[:, lanes].astype(F32)
+        both = both_ref[:, row * 2 * share : (row + 1) * 2 * share, :].astype(F32)
+        gradient = seed_ref[:, lanes].astype(F32) + proj_adjoint_row(
+            row,
+            both,
+            pair,
+            grad_gate_in_ref[:, lanes],
+            gates_in_t_ref,
+            gates_in_ref,
+            normal_ref,
+            proj_ref,
+            width,
+        )
+        grad_ref[:, lanes] = gradient
+        tri = received[:, row * share : (row + 1) * share, :].reshape(width, LANES)
+        unit, scaled, _, _, grad_tri, grad_gate = tri_adjoint_row(
+            tri,
+            pair_out_ref[:, lanes].astype(F32),
+            gradient,
+            gates_out_t_ref,
+            final_out_ref,
+            final_out_t_ref,
+            width,
+        )
+        unit_ref[:, lanes] = unit
+        scaled_ref[:, lanes] = scaled
+        grad_gate_ref[:, lanes] = grad_gate
+        grads_ref[:, row * share : (row + 1) * share, :] = dealt(grad_tri, groups)
+    place = rows * share
+    place = deal_rows(grads_ref, place, nt(normal_ref[...], proj_ref[...]), groups)
+    place = deal_rows(grads_ref, place, final_in_sum_ref[...], groups)
+    deal_rows(grads_ref, place, nt(unit_ref[...], scaled_ref[...]), groups)
+    send_ref[...] = grads_ref[...].astype(BF16)
+
+
+def gathered_rows(rest, start, tiles, width):
+    out = []
+    share = width // rest.shape[0]
+    for tile in range(tiles):
+        out.append(rest[:, start + tile * share : start + (tile + 1) * share, :].reshape(width, LANES))
+    return out, start + tiles * share
+
+
+def close_kernel(
+    sizes,
+    both_ref,
+    pair_ref,
+    grad_ref,
+    grad_gate_ref,
+    gates_t_ref,
+    gates_ref,
+    outer_ref,
+    final_ref,
+    spread_ref,
+    left_ref,
+    msa_normal_ref,
+    send_ref,
+    adjoint_ref,
+    left_grad_ref,
+    proj_in_ref,
+    final_in_ref,
+    final_out_ref,
+    grads_ref,
+    normal_ref,
+    proj_ref,
+    adjoint_t_ref,
+    outer_grad_ref,
+    right_grad_ref,
+):
+    rows, residues, depth, hidden, groups, width = sizes
+    share = width // groups
+    half = hidden // 2
+    for row in range(rows):
+        lanes = slice(row * LANES, (row + 1) * LANES)
+        both = both_ref[:, row * 2 * share : (row + 1) * 2 * share, :].astype(F32)
+        gradient = grad_ref[:, lanes] + proj_adjoint_row(
+            row,
+            both,
+            pair_ref[:, lanes].astype(F32),
+            grad_gate_ref[:, lanes],
+            gates_t_ref,
+            gates_ref,
+            normal_ref,
+            proj_ref,
+            width,
+        )
+        adjoint = gradient.astype(BF16)
+        adjoint_t_ref[:, lanes] = adjoint
+        adjoint_ref[row] = adjoint.astype(F32).T[:residues].astype(BF16)
+        spread_grad = nn(final_ref[...], adjoint).astype(BF16)
+        for h in range(2):
+            for d in range(half):
+                at = (h * half + d) * hidden
+                to = (h * rows + row) * hidden
+                outer_grad_ref[to : to + hidden, d * LANES : (d + 1) * LANES] = spread_grad[
+                    at : at + hidden
+                ]
+    for d in range(half):
+        piece = tn(outer_grad_ref[:, d * LANES : (d + 1) * LANES], left_ref[...]) / depth
+        right_grad_ref[pl.ds(d, residues, stride=half), :] = piece[:residues]
+    own = rows * half
+    grads_ref[:, :own, :] = right_grad_ref[...].reshape(groups, own, LANES)
+    place = deal_rows(grads_ref, own, nt(normal_ref[...], proj_ref[...]), groups)
+    outer_sum = nt(outer_ref[...], adjoint_t_ref[...])
+    place = deal_rows(grads_ref, place, outer_sum, groups)
+    stacked = nn(outer_grad_ref[...], spread_ref[...]) / depth
+    count = rows * hidden
+    lane = lax.broadcasted_iota(jnp.int32, (count, LANES), 1)
+    left_grad = jnp.where(
+        lane < depth, stacked[:count] + pltpu.roll(stacked[count:], LANES - depth, 1), 0.0
+    ).astype(BF16)
+    left_grad_ref[...] = left_grad
+    flank = jnp.zeros((hidden, msa_normal_ref.shape[2]), F32)
+    for row in range(rows):
+        flank = flank + nn(
+            left_grad[row * hidden : (row + 1) * hidden, :depth], msa_normal_ref[row]
+        )
+    for tile in range(flank.shape[1] // LANES):
+        part = flank[:, tile * LANES : (tile + 1) * LANES].reshape(hidden // SUB, SUB, LANES)
+        spare = tile * (hidden // SUB)
+        grads_ref[spare : spare + hidden // SUB, place : place + SUB, :] = part
+    used = (flank.shape[1] // LANES) * (hidden // SUB)
+    grads_ref[used:, place : place + SUB, :] = jnp.zeros((groups - used, SUB, LANES), F32)
+    send_ref[...] = grads_ref[...].astype(BF16)
+    rest = both_ref[:, rows * 2 * share :, :].astype(F32)
+    tiles, place = gathered_rows(rest, 0, proj_in_ref.shape[1] // LANES, width)
+    for tile, value in enumerate(tiles):
+        proj_in_ref[:, tile * LANES : (tile + 1) * LANES] = value / residues
+    tiles, place = gathered_rows(rest, place, 1, width)
+    final_in_ref[...] = tiles[0] / residues
+    tiles, place = gathered_rows(rest, place, 1, width)
+    final_out_ref[...] = tiles[0] / residues
+
+
+def msa_adjoint_kernel(
+    sizes,
+    parts_ref,
+    left_grad_ref,
+    msa_ref,
+    msa_normal_ref,
+    flank_t_ref,
+    send_ref,
+    adjoint_ref,
+):
+    rows, depth, hidden, groups = sizes
+    half = hidden // 2
+    own = rows * half
+    summed = jnp.sum(parts_ref[...].astype(F32), axis=0).astype(BF16)
+    right = summed[:own].astype(F32)
+    flank = jnp.zeros((hidden, msa_normal_ref.shape[2]), F32)
+    for row in range(rows):
+        part = right[row * half : (row + 1) * half]
+        right_grad = jnp.concatenate([part, pltpu.roll(part, LANES - depth, 1)], axis=0)[
+            :, :depth
+        ].astype(BF16)
+        left_grad = left_grad_ref[row * hidden : (row + 1) * hidden, :depth]
+        flank = flank + nn(right_grad, msa_normal_ref[row])
+        grad = jnp.concatenate([left_grad, right_grad], axis=0)
+        gradient = tn(grad, flank_t_ref[...])
+        hatted, factor = moments(msa_ref[row].astype(F32), 1)
+        adjoint_ref[row] = moments_adjoint(hatted, factor, gradient, 1).astype(BF16)
+    rest = summed[own:]
+    flank = flank.astype(BF16)
+    for group in range(groups):
+        send_ref[group, : rest.shape[0], :] = rest
+        for tile in range(flank.shape[1] // LANES):
+            at = rest.shape[0] + tile * hidden
+            send_ref[group, at : at + hidden, :] = flank[:, tile * LANES : (tile + 1) * LANES]
+
+
+def totals_kernel(sizes, parts_ref, proj_ref, final_ref, flank_ref, wide_ref):
+    residues, hidden, groups, width = sizes
+    parts = parts_ref[...].astype(F32)
+    tiles, place = gathered_rows(parts, 0, proj_ref.shape[1] // LANES, width)
+    for tile, value in enumerate(tiles):
+        proj_ref[:, tile * LANES : (tile + 1) * LANES] = value / residues
+    share = wide_ref.shape[0] // groups
+    wide_ref[...] = parts[:, place : place + share, :].reshape(wide_ref.shape) / residues
+    for c in range(hidden):
+        final_ref[c * hidden : (c + 1) * hidden, :] = wide_ref[pl.ds(c, hidden, stride=hidden), :]
+    place += share
+    blocks = hidden // SUB
+    for tile in range(flank_ref.shape[1] // LANES):
+        lanes = slice(tile * LANES, (tile + 1) * LANES)
+        left = parts[tile * blocks : (tile + 1) * blocks, place : place + SUB, :]
+        flank_ref[:hidden, lanes] = left.reshape(hidden, LANES) / residues
+        at = place + SUB + tile * hidden
+        flank_ref[hidden:, lanes] = jnp.sum(parts[:, at : at + hidden, :], axis=0) / residues
+
+
+def kernel_shards(
+    edge_embedding,
+    alignment_embedding,
+    tensor_flank_matrix,
+    tensor_final_matrix,
+    outward_sigmoid_matrix,
+    outward_final_matrix,
+    inward_sigmoid_matrix,
+    inward_final_matrix,
+    adjoint_seed,
+):
+    groups = lax.axis_size("dap")
+    rows, residues, width = edge_embedding.shape
+    depth, _, features = alignment_embedding.shape
+    hidden = tensor_flank_matrix.shape[1] // 2
+    half = hidden // 2
+    share = width // groups
+    spots = rows * LANES
+    square = hidden * hidden
+
+    def shape(*dims, dtype=BF16):
+        return jax.ShapeDtypeStruct(dims, dtype)
+
+    msa = jnp.swapaxes(alignment_embedding, 0, 1)
+    flank_t = tensor_flank_matrix.T
+    send, msa_normal, left = launch(
+        partial(msa_kernel, (rows, depth, hidden, groups)),
+        [
+            shape(groups, rows * half, LANES),
+            shape(rows, depth, features),
+            shape(2 * rows * hidden, LANES),
+        ],
+        (msa, flank_t),
+        name="msa",
+    )
+    right = exchanged(send)
+
+    final_sorted = (
+        tensor_final_matrix.reshape(hidden, hidden, width).swapaxes(0, 1).reshape(square, width)
+    )
+    final_sorted_t = final_sorted.T
+    gates_out_t = outward_sigmoid_matrix.T
+    gates_in_t = inward_sigmoid_matrix.T
+    final_out_t = outward_final_matrix.T
+    final_in_t = inward_final_matrix.T
+
+    send, spread, outer, pair_one = launch(
+        partial(outer_kernel, (rows, residues, depth, hidden, groups, width)),
+        [
+            shape(groups, rows * 2 * share, LANES),
+            shape(half * LANES, LANES),
+            shape(square, spots),
+            shape(width, spots),
+        ],
+        (right, left, edge_embedding, final_sorted_t, gates_out_t),
+        [pltpu.VMEM((residues * half, LANES), F32)],
+        name="outer",
+    )
+
+    def triangle(both, outgoing):
+        return launch(
+            partial(triangle_kernel, (residues, share), outgoing),
+            [shape(groups, rows * share, LANES)],
+            (both,),
+            [
+                pltpu.VMEM((residues * 2 * share, LANES), F32),
+                pltpu.VMEM((residues * share, LANES), F32),
+            ],
+            name="triangle_out" if outgoing else "triangle_in",
+        )[0]
+
+    def triangle_adjoint(both, grads, outgoing):
+        riders = grads.shape[1] - rows * share
+        return launch(
+            partial(triangle_adjoint_kernel, (residues, share, rows, riders), outgoing),
+            [shape(groups, rows * 2 * share + riders, LANES)],
+            (both, grads),
+            [
+                pltpu.VMEM((residues * 2 * share, LANES), F32),
+                pltpu.VMEM((residues * share, LANES), F32),
+                pltpu.VMEM((residues * 2 * share, LANES), F32),
+            ],
+            name="adjoint_out" if outgoing else "adjoint_in",
+        )[0]
+
+    both_out = exchanged(send)
+    tri_out = exchanged(triangle(both_out, True))
+    send, pair_two = launch(
+        partial(middle_kernel, (rows, groups, width)),
+        [shape(groups, rows * 2 * share, LANES), shape(width, spots)],
+        (tri_out, pair_one, gates_out_t, final_out_t, gates_in_t),
+        name="middle",
+    )
+    both_in = exchanged(send)
+    tri_in = exchanged(triangle(both_in, False))
+    send, updated, seed_t, grad_gate_in, final_in_sum = launch(
+        partial(turn_kernel, (rows, residues, groups, width)),
+        [
+            shape(groups, rows * share, LANES),
+            shape(rows, residues, width),
+            shape(width, spots),
+            shape(width, spots),
+            shape(width, width, dtype=F32),
+        ],
+        (tri_in, pair_two, adjoint_seed, gates_in_t, inward_final_matrix, final_in_t),
+        [
+            pltpu.VMEM((groups, rows * share, LANES), F32),
+            pltpu.VMEM((width, spots), BF16),
+            pltpu.VMEM((width, spots), BF16),
+        ],
+        name="turn",
+    )
+    grads = exchanged(triangle_adjoint(both_in, exchanged(send), False))
+    riders = share * (gates_in_t.shape[0] // LANES + 2)
+    send, grad_two, grad_gate_out = launch(
+        partial(between_kernel, (rows, groups, width)),
+        [
+            shape(groups, rows * share + riders, LANES),
+            shape(width, spots, dtype=F32),
+            shape(width, spots),
+        ],
+        (
+            grads,
+            pair_two,
+            seed_t,
+            grad_gate_in,
+            gates_in_t,
+            inward_sigmoid_matrix,
+            final_in_sum,
+            tri_out,
+            pair_one,
+            gates_out_t,
+            outward_final_matrix,
+            final_out_t,
+        ),
+        [
+            pltpu.VMEM((groups, rows * share + riders, LANES), F32),
+            pltpu.VMEM((width, spots), BF16),
+            pltpu.VMEM((5 * width, spots), BF16),
+            pltpu.VMEM((width, spots), BF16),
+            pltpu.VMEM((width, spots), BF16),
+        ],
+        name="between",
+    )
+    grads = exchanged(triangle_adjoint(both_out, exchanged(send), True))
+    count = rows * half + share * 5 + square // groups + SUB
+    send, edge_adjoint, left_grad, proj_in, final_in, final_out = launch(
+        partial(close_kernel, (rows, residues, depth, hidden, groups, width)),
+        [
+            shape(groups, count, LANES),
+            shape(rows, residues, width),
+            shape(rows * hidden, LANES),
+            shape(width, 5 * width, dtype=F32),
+            shape(width, width, dtype=F32),
+            shape(width, width, dtype=F32),
+        ],
+        (
+            grads,
+            pair_one,
+            grad_two,
+            grad_gate_out,
+            gates_out_t,
+            outward_sigmoid_matrix,
+            outer,
+            final_sorted,
+            spread,
+            left,
+            msa_normal,
+        ),
+        [
+            pltpu.VMEM((groups, count, LANES), F32),
+            pltpu.VMEM((width, spots), BF16),
+            pltpu.VMEM((5 * width, spots), BF16),
+            pltpu.VMEM((width, spots), BF16),
+            pltpu.VMEM((2 * rows * hidden, half * LANES), BF16),
+            pltpu.VMEM((residues * half, LANES), F32),
+        ],
+        name="close",
+    )
+    rest = count - rows * half
+    send, msa_adjoint = launch(
+        partial(msa_adjoint_kernel, (rows, depth, hidden, groups)),
+        [
+            shape(groups, rest + hidden * features // LANES, LANES),
+            shape(rows, depth, features),
+        ],
+        (exchanged(send), left_grad, msa, msa_normal, flank_t),
+        name="msa_adjoint",
+    )
+    proj_out, outer_final, outer_proj_t = launch(
+        partial(totals_kernel, (residues, hidden, groups, width)),
+        [
+            shape(width, 5 * width, dtype=F32),
+            shape(square, width, dtype=F32),
+            shape(2 * hidden, features, dtype=F32),
+        ],
+        (exchanged(send),),
+        [pltpu.VMEM((square, width), F32)],
+        name="totals",
+    )
+    return (
+        updated,
+        edge_adjoint,
+        jnp.swapaxes(msa_adjoint, 0, 1),
+        outer_proj_t.T,
+        outer_final,
+        proj_out,
+        final_out,
+        proj_in,
+        final_in,
+    )
+
+
+def any_shards(edge_embedding, alignment_embedding, tensor_flank_matrix, *others):
+    groups = lax.axis_size("dap")
+    rows, residues, width = edge_embedding.shape
+    depth, _, features = alignment_embedding.shape
+    hidden = tensor_flank_matrix.shape[1] // 2
+    fits = (
+        width == LANES
+        and others[2].shape[0] == width
+        and width % (groups * SUB) == 0
+        and residues <= LANES
+        and residues % SUB == 0
+        and (rows * hidden // 2) % 16 == 0
+        and (rows * width // groups) % 16 == 0
+        and 2 * depth == LANES
+        and hidden == 32
+        and features % LANES == 0
+        and (features // LANES) * (hidden // SUB) <= groups
+        and hidden * hidden % (groups * SUB) == 0
+    )
+    program = kernel_shards if fits else shards
+    return program(edge_embedding, alignment_embedding, tensor_flank_matrix, *others)
+
+
 def solution(mesh):
     placed = (
         P(("dp", "dap"), None, None),
@@ -398,7 +1149,7 @@
         P(("dp", "dap"), None, None),
     )
     return jax.shard_map(
-        shards,
+        any_shards,
         mesh=mesh,
         in_specs=placed,
         out_specs=(

time: 257 us -> 195 us (0.76)
  local copies, waits for them, and re-layouts: 50.1 us -> 9.44 us
  blocking collectives: 80.6 us -> 121 us
  matrix products: 22.9 us -> 0 us
  starting transfers between devices: 37.9 us -> 16.1 us
  other arithmetic: 21.7 us -> 0 us
  Pallas kernels: 0 us -> 19.8 us
  waiting for transfers between devices: 39.7 us -> 26.5 us
    all_to_all x6 -> x8, blocking collectives: 80.6 us -> 121 us  [exchanged(): lax.all_to_all(values, 'dap', split_axis=0, concat_axis=0, tiled=True)]
    all_to_all x4 -> x0, waiting for transfers between devices: 26.9 us -> none  [the longest x3 23.9 us: gathered(): lax.all_to_all(copies, 'dap', 0, 0, tiled=True)]
    dot_general x34 -> x0, matrix products: 22.9 us -> none  [the longest x2 3.86 us: sigmoid_pieces(): jnp.dot(standardized_edges, linear_mapping[:, 4 * latent_tensor:], prefer...]
    all_to_all x4 -> x0, starting transfers between devices: 20 us -> none  [the longest x3 16.2 us: gathered(): lax.all_to_all(copies, 'dap', 0, 0, tiled=True)]
    pallas_call x0 -> x12, Pallas kernels: none -> 19.8 us  [launch(): pl.pallas_call(body, out_shape=outs, in_specs=[vmem] * len(args), out_spe...]
    all_to_all x3, waiting for transfers between devices: 12.8 us -> 26.5 us  [exchanged(): lax.all_to_all(values, 'dap', split_axis=0, concat_axis=0, tiled=True)]
    convert_element_type x18 -> x0, other arithmetic: 10.6 us -> none  [the longest x13 7.83 us: truncated_numbers(): return lax.optimization_barrier(values.astype(jnp.bfloat16))]
    convert_element_type x11 -> x0, local copies, waits for them, and re-layouts: 9.66 us -> none  [the longest x8 6.62 us: triangle_back(): values.astype(jnp.float32)]
  transfers between devices with their start and end apart: 7 -> 3, of which waited for: 6 -> 3; matrix products, arithmetic and copies ran while one was open for 13% -> 1% of each run, Pallas kernels for 0% -> 0%
where the time goes in v2:
time: 195 us; the launch traced here: 194 us
  blocking collectives  121 us (62%)
  waiting for transfers between devices  26.5 us (14%)
  Pallas kernels  19.8 us (10%)
  starting transfers between devices  16.1 us (8%)
  local copies, waits for them, and re-layouts  9.44 us (5%)
    all_to_all x8, blocking collectives, exchanged(): lax.all_to_all(values, 'dap', split_axis=0, concat_axis=0, tiled=True)  121 us
    all_to_all x3, waiting for transfers between devices, exchanged(): lax.all_to_all(values, 'dap', split_axis=0, concat_axis=0, tiled=True)  26.5 us
    pallas_call x12, Pallas kernels, launch(): pl.pallas_call(body, out_shape=outs, in_specs=[vmem] * len(args), out_spe...  19.8 us
    all_to_all x3, starting transfers between devices, exchanged(): lax.all_to_all(values, 'dap', split_axis=0, concat_axis=0, tiled=True)  16.1 us
    unnamed x54, local copies, waits for them, and re-layouts  9.19 us
  transfers between devices with their start and end apart: 3, of which 3 were waited for; matrix products, arithmetic and copies ran while one was open for 1% of the time, Pallas kernels for 0%

profile of v2, /device:TPU:0, one launch (start us, length us, event | category | flops | bytes accessed | tf_op | source)
XLA Modules:
  0.0 193.6 jit_solution(7799257385250056889)
XLA Ops:
  2.4 1.2 msa.1
  3.6 8.3 %all-to-all-start = ((bf16[16,96,128]{2,1,0:T(8,128)(2,1)}), bf16[16,96,128]{2,1,0:T(8,128)(2,1)S(1)}, u32[]{:S(2)}, u32[]{:S(2)}) async-start(bf16[16,96,128]{2,1,0:T(8,128)(2,1)} %get-tuple-element.37), calls=%async_computation | async-start | bytes 786432 | tf_op jit(solution)/shard_map/all_to_all | solution.py:70
  12.4 12.2 %all-to-all-done.right_ref = bf16[16,96,128]{2,1,0:T(8,128)(2,1)S(1)} async-done(((bf16[16,96,128]{2,1,0:T(8,128)(2,1)}), bf16[16,96,128]{2,1,0:T(8,128)(2,1)S(1)}, u32[]{:S(2)}, u32[]{:S(2)}) %all-to-all-start) | async-done | bytes 393248 | tf_op jit(solution)/shard_map/all_to_all | solution.py:70
  24.6 1.4 outer.1
  26.8 15.4 %all_to_all.55.both_ref = bf16[16,96,128]{2,1,0:T(8,128)(2,1)S(1)} all-to-all(bf16[16,96,128]{2,1,0:T(8,128)(2,1)S(1)} %get-tuple-element.39), channel_id=1, replica_groups=mesh['dap'=16,'dp'=2] {'dap'}, dimensions={0} | all-to-all | bytes 786432 | tf_op jit(solution)/shard_map/all_to_all | solution.py:70
  42.2 1.1 triangle_out.1
  43.3 3.6 %all-to-all-start.2 = ((bf16[16,48,128]{2,1,0:T(8,128)(2,1)}), bf16[16,48,128]{2,1,0:T(8,128)(2,1)S(1)}, u32[]{:S(2)}, u32[]{:S(2)}) async-start(bf16[16,48,128]{2,1,0:T(8,128)(2,1)} %triangle_out.1), calls=%async_computation.2 | async-start | bytes 393216 | tf_op jit(solution)/shard_map/all_to_all | solution.py:70
  47.2 7.8 %all-to-all-done.2.tri_ref = bf16[16,48,128]{2,1,0:T(8,128)(2,1)S(1)} async-done(((bf16[16,48,128]{2,1,0:T(8,128)(2,1)}), bf16[16,48,128]{2,1,0:T(8,128)(2,1)S(1)}, u32[]{:S(2)}, u32[]{:S(2)}) %all-to-all-start.2) | async-done | bytes 196640 | tf_op jit(solution)/shard_map/all_to_all | solution.py:70
  55.0 1.2 middle.1
  56.9 13.2 %all_to_all.56.both_ref = bf16[16,96,128]{2,1,0:T(8,128)(2,1)S(1)} all-to-all(bf16[16,96,128]{2,1,0:T(8,128)(2,1)S(1)} %get-tuple-element.41), channel_id=1, replica_groups=mesh['dap'=16,'dp'=2] {'dap'}, dimensions={0} | all-to-all | bytes 786432 | tf_op jit(solution)/shard_map/all_to_all | solution.py:70
  71.2 4.2 %all-to-all-start.4 = ((bf16[16,48,128]{2,1,0:T(8,128)(2,1)}), bf16[16,48,128]{2,1,0:T(8,128)(2,1)}, u32[]{:S(2)}, u32[]{:S(2)}) async-start(bf16[16,48,128]{2,1,0:T(8,128)(2,1)} %copy-done.13), calls=%async_computation.4 | async-start | bytes 393216 | tf_op jit(solution)/shard_map/all_to_all | solution.py:70
  75.3 1.5 copy.23
  76.8 6.6 %all-to-all-done.4.tri_ref = bf16[16,48,128]{2,1,0:T(8,128)(2,1)} async-done(((bf16[16,48,128]{2,1,0:T(8,128)(2,1)}), bf16[16,48,128]{2,1,0:T(8,128)(2,1)}, u32[]{:S(2)}, u32[]{:S(2)}) %all-to-all-start.4) | async-done | bytes 196640 | tf_op jit(solution)/shard_map/all_to_all | solution.py:70
  86.8 2.9 %turn.1 = (bf16[16,48,128]{2,1,0:T(8,128)(2,1)S(1)}, bf16[6,96,128]{2,1,0:T(8,128)(2,1)}, bf16[128,768]{1,0:T(8,128)(2,1)S(1)}, bf16[128,768]{1,0:T(8,128)(2,1)S(1)}, f32[128,128]{1,0:T(8,128)S(1)}) custom-call(bf16[16,48,128]{2,1,0:T(8,128)(2,1)} %all-to-all-done.4.tri_ref, bf16[128,768]{1,0:T(8,128)(2,1)S(1)} %copy-done.1, ...), custom_call_target="tpu_custom_call" | custom-call | flops 200000000 | bytes 1572864 | tf_op jit(solution)/shard_map/turn/pallas_call | solution.py:415
  89.7 11.0 %all_to_all.57.grad_ref = bf16[16,48,128]{2,1,0:T(8,128)(2,1)S(1)} all-to-all(bf16[16,48,128]{2,1,0:T(8,128)(2,1)S(1)} %get-tuple-element.44), channel_id=1, replica_groups=mesh['dap'=16,'dp'=2] {'dap'}, dimensions={0} | all-to-all | bytes 393216 | tf_op jit(solution)/shard_map/all_to_all | solution.py:70
  101.4 12.7 %all_to_all.58.both_ref = bf16[16,96,128]{2,1,0:T(8,128)(2,1)S(1)} all-to-all(bf16[16,96,128]{2,1,0:T(8,128)(2,1)S(1)} %adjoint_in.1), channel_id=1, replica_groups=mesh['dap'=16,'dp'=2] {'dap'}, dimensions={0} | all-to-all | bytes 786432 | tf_op jit(solution)/shard_map/all_to_all | solution.py:70
  114.0 2.3 %between.1 = (bf16[16,104,128]{2,1,0:T(8,128)(2,1)S(1)}, f32[128,768]{1,0:T(8,128)S(1)}, bf16[128,768]{1,0:T(8,128)(2,1)S(1)}) custom-call(bf16[16,96,128]{2,1,0:T(8,128)(2,1)S(1)} %all_to_all.58.both_ref, bf16[128,768]{1,0:T(8,128)(2,1)S(1)} %copy-done.2, bf16[128,768]{1,0:T(8,128)(2,1)S(1)} %get-tuple-element.45.seed_ref, ...), custom_call_target="tpu_custom_call" | custom-call | flops 200000000 | bytes 3014656 | tf_op jit(solution)/shard_map/between/pallas_call | solution.py:415
  116.4 13.8 %all_to_all.59.grad_ref = bf16[16,104,128]{2,1,0:T(8,128)(2,1)S(1)} all-to-all(bf16[16,104,128]{2,1,0:T(8,128)(2,1)S(1)} %get-tuple-element.48), channel_id=1, replica_groups=mesh['dap'=16,'dp'=2] {'dap'}, dimensions={0} | all-to-all | bytes 851968 | tf_op jit(solution)/shard_map/all_to_all | solution.py:70
  130.9 16.4 %all_to_all.60.both_ref = bf16[16,152,128]{2,1,0:T(8,128)(2,1)S(1)} all-to-all(bf16[16,152,128]{2,1,0:T(8,128)(2,1)S(1)} %adjoint_out.1), channel_id=1, replica_groups=mesh['dap'=16,'dp'=2] {'dap'}, dimensions={0} | all-to-all | bytes 1245184 | tf_op jit(solution)/shard_map/all_to_all | solution.py:70
  147.3 5.2 %close.1 = (bf16[16,208,128]{2,1,0:T(8,128)(2,1)S(1)}, bf16[6,96,128]{2,1,0:T(8,128)(2,1)}, bf16[192,128]{1,0:T(8,128)(2,1)S(1)}, f32[128,640]{1,0:T(8,128)}, f32[128,128]{1,0:T(8,128)}, /*index=5*/f32[128,128]{1,0:T(8,128)}) custom-call(bf16[16,152,128]{2,1,0:T(8,128)(2,1)S(1)} %all_to_all.60.both_ref, ...), custom_call_target="tpu_custom_call" | custom-call | flops 200000000 | bytes 5898240 | tf_op jit(solution)/shard_map/close/pallas_call | solution.py:415
  152.5 17.9 %all_to_all.61.parts_ref = bf16[16,208,128]{2,1,0:T(8,128)(2,1)S(1)} all-to-all(bf16[16,208,128]{2,1,0:T(8,128)(2,1)S(1)} %get-tuple-element.55), channel_id=1, replica_groups=mesh['dap'=16,'dp'=2] {'dap'}, dimensions={0} | all-to-all | bytes 1703936 | tf_op jit(solution)/shard_map/all_to_all | solution.py:70
  170.4 1.4 msa_adjoint.1
  171.8 20.5 %all_to_all.62.parts_ref = bf16[16,176,128]{2,1,0:T(8,128)(2,1)S(1)} all-to-all(bf16[16,176,128]{2,1,0:T(8,128)(2,1)S(1)} %get-tuple-element.58), channel_id=1, replica_groups=mesh['dap'=16,'dp'=2] {'dap'}, dimensions={0} | all-to-all | bytes 1441792 | tf_op jit(solution)/shard_map/all_to_all | solution.py:70
  192.4 1.3 totals.1
  (58 shorter events, 9.8 us)
Async XLA Ops:
  0.6 11.3 %copy-start.3 = (bf16[128,640]{1,0:T(8,128)(2,1)S(1)}, bf16[128,640]{1,0:T(8,128)(2,1)}, u32[]{:S(2)}) copy-start(bf16[128,640]{1,0:T(8,128)(2,1)} %gates_ref.1) | copy-start | bytes 491524
  0.7 1.0 copy-start.14
  1.6 0.8 copy-start.22
  2.4 9.8 %copy-start.24 = (bf16[1024,128]{1,0:T(8,128)(2,1)S(1)}, bf16[1024,128]{1,0:T(8,128)(2,1)}, u32[]{:S(2)}) copy-start(bf16[1024,128]{1,0:T(8,128)(2,1)} %param.12) | copy-start | bytes 786436
  2.4 22.2 %copy-start.16 = (bf16[6,96,128]{2,1,0:T(8,128)(2,1)S(1)}, bf16[6,96,128]{2,1,0:T(8,128)(2,1)}, u32[]{:S(2)}) copy-start(bf16[6,96,128]{2,1,0:T(8,128)(2,1)} %edge_ref.1) | copy-start | bytes 442372
  3.6 22.4 %copy-start.9 = (bf16[384,128]{1,0:T(8,128)(2,1)}, bf16[384,128]{1,0:T(8,128)(2,1)S(1)}, u32[]{:S(2)}) copy-start(bf16[384,128]{1,0:T(8,128)(2,1)S(1)} %get-tuple-element.38.left_ref) | copy-start | bytes 294916
  3.6 21.0 %all-to-all-start = ((bf16[16,96,128]{2,1,0:T(8,128)(2,1)}), bf16[16,96,128]{2,1,0:T(8,128)(2,1)S(1)}, u32[]{:S(2)}, u32[]{:S(2)}) async-start(bf16[16,96,128]{2,1,0:T(8,128)(2,1)} %get-tuple-element.37), calls=%async_computation | async-start | bytes 786432 | tf_op jit(solution)/shard_map/all_to_all | solution.py:70
  12.4 34.5 %copy-start.18 = (bf16[128,128]{1,0:T(8,128)(2,1)S(1)}, bf16[128,128]{1,0:T(8,128)(2,1)}, u32[]{:S(2)}) copy-start(bf16[128,128]{1,0:T(8,128)(2,1)} %final_out_ref.1) | copy-start | bytes 98308
  12.4 34.7 %copy-start.5 = (bf16[128,640]{1,0:T(8,128)(2,1)S(1)}, bf16[128,640]{1,0:T(8,128)(2,1)}, u32[]{:S(2)}) copy-start(bf16[128,640]{1,0:T(8,128)(2,1)} %gates_in_ref.1) | copy-start | bytes 491524
  26.0 0.8 copy-start.7
  43.3 11.7 %all-to-all-start.2 = ((bf16[16,48,128]{2,1,0:T(8,128)(2,1)}), bf16[16,48,128]{2,1,0:T(8,128)(2,1)S(1)}, u32[]{:S(2)}, u32[]{:S(2)}) async-start(bf16[16,48,128]{2,1,0:T(8,128)(2,1)} %triangle_out.1), calls=%async_computation.2 | async-start | bytes 393216 | tf_op jit(solution)/shard_map/all_to_all | solution.py:70
  47.1 9.1 %copy-start.11 = (bf16[128,128]{0,1:T(8,128)(2,1)}, bf16[128,128]{0,1:T(8,128)(2,1)S(1)}, u32[]{:S(2)}) copy-start(bf16[128,128]{0,1:T(8,128)(2,1)S(1)} %copy.21) | copy-start | bytes 98308
  71.2 12.3 %all-to-all-start.4 = ((bf16[16,48,128]{2,1,0:T(8,128)(2,1)}), bf16[16,48,128]{2,1,0:T(8,128)(2,1)}, u32[]{:S(2)}, u32[]{:S(2)}) async-start(bf16[16,48,128]{2,1,0:T(8,128)(2,1)} %copy-done.13), calls=%async_computation.4 | async-start | bytes 393216 | tf_op jit(solution)/shard_map/all_to_all | solution.py:70
  83.4 0.9 copy-start.1
  84.4 0.9 copy-start.17
  86.8 27.2 %copy-start.2 = (bf16[128,768]{1,0:T(8,128)(2,1)S(1)}, bf16[128,768]{1,0:T(8,128)(2,1)}, u32[]{:S(2)}) copy-start(bf16[128,768]{1,0:T(8,128)(2,1)} %copy-done) | copy-start | bytes 589828
  86.8 27.2 %copy-start.6 = (bf16[128,640]{1,0:T(8,128)(2,1)S(1)}, bf16[128,640]{1,0:T(8,128)(2,1)}, u32[]{:S(2)}) copy-start(bf16[128,640]{1,0:T(8,128)(2,1)} %gates_in_ref.1) | copy-start | bytes 491524
  86.8 27.2 %copy-start.12 = (bf16[128,128]{0,1:T(8,128)(2,1)S(1)}, bf16[128,128]{0,1:T(8,128)(2,1)}, u32[]{:S(2)}) copy-start(bf16[128,128]{0,1:T(8,128)(2,1)} %copy-done.11) | copy-start | bytes 98308
  86.8 27.2 %copy-start.19 = (bf16[128,128]{1,0:T(8,128)(2,1)S(1)}, bf16[128,128]{1,0:T(8,128)(2,1)}, u32[]{:S(2)}) copy-start(bf16[128,128]{1,0:T(8,128)(2,1)} %final_out_ref.1) | copy-start | bytes 98308
  116.3 30.9 %copy-start.4 = (bf16[128,640]{1,0:T(8,128)(2,1)S(1)}, bf16[128,640]{1,0:T(8,128)(2,1)}, u32[]{:S(2)}) copy-start(bf16[128,640]{1,0:T(8,128)(2,1)} %gates_ref.1) | copy-start | bytes 491524
  116.3 30.9 %copy-start.8 = (bf16[2048,128]{1,0:T(8,128)(2,1)S(1)}, bf16[2048,128]{1,0:T(8,128)(2,1)}, u32[]{:S(2)}) copy-start(bf16[2048,128]{1,0:T(8,128)(2,1)} %copy-done.7) | copy-start | bytes 1572868
  116.4 30.9 %copy-start.10 = (bf16[384,128]{1,0:T(8,128)(2,1)S(1)}, bf16[384,128]{1,0:T(8,128)(2,1)}, u32[]{:S(2)}) copy-start(bf16[384,128]{1,0:T(8,128)(2,1)} %copy-done.9) | copy-start | bytes 294916
  152.5 17.9 %copy-start.15 = (bf16[64,6,256]{2,0,1:T(8,128)(2,1)S(1)}, bf16[64,6,256]{2,0,1:T(8,128)(2,1)}, u32[]{:S(2)}) copy-start(bf16[64,6,256]{2,0,1:T(8,128)(2,1)} %param.10) | copy-start | bytes 589828
  152.5 17.9 %copy-start.23 = (bf16[256,64]{0,1:T(8,128)(2,1)S(1)}, bf16[256,64]{0,1:T(8,128)(2,1)}, u32[]{:S(2)}) copy-start(bf16[256,64]{0,1:T(8,128)(2,1)} %param.11) | copy-start | bytes 98308
  (4 other events, 2.9 us)

commit v3 on v2

--- a/solution.py
+++ b/solution.py
@@ -422,7 +422,7 @@
         cost_estimate=pl.CostEstimate(
             flops=int(flops), bytes_accessed=int(moved), transcendentals=0
         ),
-        compiler_params=pltpu.CompilerParams(vmem_limit_bytes=40 * 1024 * 1024),
+        compiler_params=pltpu.CompilerParams(vmem_limit_bytes=24 * 1024 * 1024),
     )(*args)
 
 
@@ -945,6 +945,11 @@
     gates_in_t = inward_sigmoid_matrix.T
     final_out_t = outward_final_matrix.T
     final_in_t = inward_final_matrix.T
+    right, final_sorted, final_sorted_t, gates_out_t, gates_in_t, final_out_t, final_in_t = (
+        lax.optimization_barrier(
+            (right, final_sorted, final_sorted_t, gates_out_t, gates_in_t, final_out_t, final_in_t)
+        )
+    )
 
     send, spread, outer, pair_one = launch(
         partial(outer_kernel, (rows, residues, depth, hidden, groups, width)),

time: 195 us -> 183 us (0.938)
  blocking collectives: 121 us -> 141 us
  waiting for transfers between devices: 26.5 us -> 11.2 us
  starting transfers between devices: 16.1 us -> 8.34 us
  local copies, waits for them, and re-layouts: 9.44 us -> 3.33 us
    all_to_all x8 -> x10, blocking collectives: 121 us -> 141 us  [exchanged(): lax.all_to_all(values, 'dap', split_axis=0, concat_axis=0, tiled=True)]
    all_to_all x3 -> x1, waiting for transfers between devices: 26.5 us -> 11.2 us  [exchanged(): lax.all_to_all(values, 'dap', split_axis=0, concat_axis=0, tiled=True)]
    all_to_all x3 -> x1, starting transfers between devices: 16.1 us -> 8.34 us  [exchanged(): lax.all_to_all(values, 'dap', split_axis=0, concat_axis=0, tiled=True)]
    unnamed x54 -> x26, local copies, waits for them, and re-layouts: 9.19 us -> 3.08 us
  transfers between devices with their start and end apart: 3 -> 1, of which waited for: 3 -> 1; matrix products, arithmetic and copies ran while one was open for 1% -> 1% of each run, Pallas kernels for 0% -> 0%
where the time goes in v3:
time: 183 us
  blocking collectives  141 us (77%)
  Pallas kernels  18.1 us (10%)
  waiting for transfers between devices  11.2 us (6%)
  starting transfers between devices  8.34 us (5%)
  local copies, waits for them, and re-layouts  3.33 us (2%)
    all_to_all x10, blocking collectives, exchanged(): lax.all_to_all(values, 'dap', split_axis=0, concat_axis=0, tiled=True)  141 us
    pallas_call x12, Pallas kernels, launch(): pl.pallas_call(body, out_shape=outs, in_specs=[vmem] * len(args), out_spe...  18.1 us
    all_to_all x1, waiting for transfers between devices, exchanged(): lax.all_to_all(values, 'dap', split_axis=0, concat_axis=0, tiled=True)  11.2 us
    all_to_all x1, starting transfers between devices, exchanged(): lax.all_to_all(values, 'dap', split_axis=0, concat_axis=0, tiled=True)  8.34 us
  transfers between devices with their start and end apart: 1, of which 1 were waited for; matrix products, arithmetic and copies ran while one was open for 1% of the time, Pallas kernels for 0%

profile of v3, /device:TPU:0, one launch (start us, length us, event | category | flops | bytes accessed | tf_op | source)
XLA Modules:
  0.0 182.6 jit_solution(11367510689899645086)
XLA Ops:
  0.7 1.0 copy-done.2
  1.6 0.8 copy-done.8
  2.4 1.2 msa.1
  3.6 8.3 %all-to-all-start = ((bf16[16,96,128]{2,1,0:T(8,128)(2,1)}), bf16[16,96,128]{2,1,0:T(8,128)(2,1)S(1)}, u32[]{:S(2)}, u32[]{:S(2)}) async-start(bf16[16,96,128]{2,1,0:T(8,128)(2,1)} %get-tuple-element.44), calls=%async_computation | async-start | bytes 786432 | tf_op jit(solution)/shard_map/all_to_all | solution.py:70
  12.0 0.9 copy.21
  13.4 11.2 %all-to-all-done.right_ref = bf16[16,96,128]{2,1,0:T(8,128)(2,1)S(1)} async-done(((bf16[16,96,128]{2,1,0:T(8,128)(2,1)}), bf16[16,96,128]{2,1,0:T(8,128)(2,1)S(1)}, u32[]{:S(2)}, u32[]{:S(2)}) %all-to-all-start) | async-done | bytes 393248 | tf_op jit(solution)/shard_map/all_to_all | solution.py:70
  24.8 1.4 outer.1
  26.2 15.4 %all_to_all.55.both_ref = bf16[16,96,128]{2,1,0:T(8,128)(2,1)S(1)} all-to-all(bf16[16,96,128]{2,1,0:T(8,128)(2,1)S(1)} %get-tuple-element.49), channel_id=1, replica_groups=mesh['dap'=16,'dp'=2] {'dap'}, dimensions={0} | all-to-all | bytes 786432 | tf_op jit(solution)/shard_map/all_to_all | solution.py:70
  42.0 11.6 %all_to_all.56.tri_ref = bf16[16,48,128]{2,1,0:T(8,128)(2,1)S(1)} all-to-all(bf16[16,48,128]{2,1,0:T(8,128)(2,1)S(1)} %triangle_out.1), channel_id=1, replica_groups=mesh['dap'=16,'dp'=2] {'dap'}, dimensions={0} | all-to-all | bytes 393216 | tf_op jit(solution)/shard_map/all_to_all | solution.py:70
  53.7 1.2 middle.1
  54.8 13.2 %all_to_all.57.both_ref = bf16[16,96,128]{2,1,0:T(8,128)(2,1)S(1)} all-to-all(bf16[16,96,128]{2,1,0:T(8,128)(2,1)S(1)} %get-tuple-element.53), channel_id=1, replica_groups=mesh['dap'=16,'dp'=2] {'dap'}, dimensions={0} | all-to-all | bytes 786432 | tf_op jit(solution)/shard_map/all_to_all | solution.py:70
  68.5 11.8 %all_to_all.58.tri_ref = bf16[16,48,128]{2,1,0:T(8,128)(2,1)S(1)} all-to-all(bf16[16,48,128]{2,1,0:T(8,128)(2,1)S(1)} %triangle_in.1), channel_id=1, replica_groups=mesh['dap'=16,'dp'=2] {'dap'}, dimensions={0} | all-to-all | bytes 393216 | tf_op jit(solution)/shard_map/all_to_all | solution.py:70
  80.2 1.9 %turn.1 = (bf16[16,48,128]{2,1,0:T(8,128)(2,1)S(1)}, bf16[6,96,128]{2,1,0:T(8,128)(2,1)}, bf16[128,768]{1,0:T(8,128)(2,1)S(1)}, bf16[128,768]{1,0:T(8,128)(2,1)S(1)}, f32[128,128]{1,0:T(8,128)S(1)}) custom-call(bf16[16,48,128]{2,1,0:T(8,128)(2,1)S(1)} %all_to_all.58.tri_ref, bf16[128,768]{1,0:T(8,128)(2,1)S(1)} %get-tuple-element.54.pair_ref.pair_in_ref, ...), custom_call_target="tpu_custom_call" | custom-call | flops 200000000 | bytes 1572864 | tf_op jit(solution)/shard_map/turn/pallas_call | solution.py:415
  82.1 11.1 %all_to_all.59.grad_ref = bf16[16,48,128]{2,1,0:T(8,128)(2,1)S(1)} all-to-all(bf16[16,48,128]{2,1,0:T(8,128)(2,1)S(1)} %get-tuple-element.57), channel_id=1, replica_groups=mesh['dap'=16,'dp'=2] {'dap'}, dimensions={0} | all-to-all | bytes 393216 | tf_op jit(solution)/shard_map/all_to_all | solution.py:70
  93.9 12.7 %all_to_all.60.both_ref = bf16[16,96,128]{2,1,0:T(8,128)(2,1)S(1)} all-to-all(bf16[16,96,128]{2,1,0:T(8,128)(2,1)S(1)} %adjoint_in.1), channel_id=1, replica_groups=mesh['dap'=16,'dp'=2] {'dap'}, dimensions={0} | all-to-all | bytes 786432 | tf_op jit(solution)/shard_map/all_to_all | solution.py:70
  106.5 2.3 %between.1 = (bf16[16,104,128]{2,1,0:T(8,128)(2,1)S(1)}, f32[128,768]{1,0:T(8,128)S(1)}, bf16[128,768]{1,0:T(8,128)(2,1)S(1)}) custom-call(bf16[16,96,128]{2,1,0:T(8,128)(2,1)S(1)} %all_to_all.60.both_ref, bf16[128,768]{1,0:T(8,128)(2,1)S(1)} %get-tuple-element.54.pair_ref.pair_in_ref, bf16[128,768]{1,0:T(8,128)(2,1)S(1)} %get-tuple-element.58.seed_ref, ...), custom_call_target="tpu_custom_call" | custom-call | flops 200000000 | bytes 3014656 | tf_op jit(solution)/shard_map/between/pallas_call | solution.py:415
  108.8 13.5 %all_to_all.61.grad_ref = bf16[16,104,128]{2,1,0:T(8,128)(2,1)S(1)} all-to-all(bf16[16,104,128]{2,1,0:T(8,128)(2,1)S(1)} %get-tuple-element.61), channel_id=1, replica_groups=mesh['dap'=16,'dp'=2] {'dap'}, dimensions={0} | all-to-all | bytes 851968 | tf_op jit(solution)/shard_map/all_to_all | solution.py:70
  122.4 0.7 adjoint_out.1
  123.1 16.5 %all_to_all.62.both_ref = bf16[16,152,128]{2,1,0:T(8,128)(2,1)S(1)} all-to-all(bf16[16,152,128]{2,1,0:T(8,128)(2,1)S(1)} %adjoint_out.1), channel_id=1, replica_groups=mesh['dap'=16,'dp'=2] {'dap'}, dimensions={0} | all-to-all | bytes 1245184 | tf_op jit(solution)/shard_map/all_to_all | solution.py:70
  139.6 5.2 %close.1 = (bf16[16,208,128]{2,1,0:T(8,128)(2,1)S(1)}, bf16[6,96,128]{2,1,0:T(8,128)(2,1)}, bf16[192,128]{1,0:T(8,128)(2,1)S(1)}, f32[128,640]{1,0:T(8,128)}, f32[128,128]{1,0:T(8,128)}, /*index=5*/f32[128,128]{1,0:T(8,128)}) custom-call(bf16[16,152,128]{2,1,0:T(8,128)(2,1)S(1)} %all_to_all.62.both_ref, ...), custom_call_target="tpu_custom_call" | custom-call | flops 200000000 | bytes 5898240 | tf_op jit(solution)/shard_map/close/pallas_call | solution.py:415
  144.8 18.2 %all_to_all.63.parts_ref = bf16[16,208,128]{2,1,0:T(8,128)(2,1)S(1)} all-to-all(bf16[16,208,128]{2,1,0:T(8,128)(2,1)S(1)} %get-tuple-element.69), channel_id=1, replica_groups=mesh['dap'=16,'dp'=2] {'dap'}, dimensions={0} | all-to-all | bytes 1703936 | tf_op jit(solution)/shard_map/all_to_all | solution.py:70
  163.0 1.4 msa_adjoint.1
  164.4 16.9 %all_to_all.64.parts_ref = bf16[16,176,128]{2,1,0:T(8,128)(2,1)S(1)} all-to-all(bf16[16,176,128]{2,1,0:T(8,128)(2,1)S(1)} %get-tuple-element.72), channel_id=1, replica_groups=mesh['dap'=16,'dp'=2] {'dap'}, dimensions={0} | all-to-all | bytes 1441792 | tf_op jit(solution)/shard_map/all_to_all | solution.py:70
  181.3 1.3 totals.1
  (28 shorter events, 2.2 us)
Async XLA Ops:
  0.6 12.3 %copy-start = (bf16[128,640]{1,0:T(8,128)(2,1)S(1)}, bf16[128,640]{1,0:T(8,128)(2,1)}, u32[]{:S(2)}) copy-start(bf16[128,640]{1,0:T(8,128)(2,1)} %gates_ref.1) | copy-start | bytes 491524
  0.7 12.5 %copy-start.1 = (bf16[128,640]{1,0:T(8,128)(2,1)S(1)}, bf16[128,640]{1,0:T(8,128)(2,1)}, u32[]{:S(2)}) copy-start(bf16[128,640]{1,0:T(8,128)(2,1)} %gates_in_ref.1) | copy-start | bytes 491524
  0.7 1.0 copy-start.2
  1.6 0.8 copy-start.8
  2.4 10.4 %copy-start.7 = (bf16[128,128]{1,0:T(8,128)(2,1)S(1)}, bf16[128,128]{1,0:T(8,128)(2,1)}, u32[]{:S(2)}) copy-start(bf16[128,128]{1,0:T(8,128)(2,1)} %final_ref.1) | copy-start | bytes 98308
  2.4 10.9 %copy-start.10 = (bf16[1024,128]{1,0:T(8,128)(2,1)S(1)}, bf16[1024,128]{1,0:T(8,128)(2,1)}, u32[]{:S(2)}) copy-start(bf16[1024,128]{1,0:T(8,128)(2,1)} %param.12) | copy-start | bytes 786436
  2.4 22.3 %copy-start.4 = (bf16[6,96,128]{2,1,0:T(8,128)(2,1)S(1)}, bf16[6,96,128]{2,1,0:T(8,128)(2,1)}, u32[]{:S(2)}) copy-start(bf16[6,96,128]{2,1,0:T(8,128)(2,1)} %edge_ref.1) | copy-start | bytes 442372
  3.6 21.0 %all-to-all-start = ((bf16[16,96,128]{2,1,0:T(8,128)(2,1)}), bf16[16,96,128]{2,1,0:T(8,128)(2,1)S(1)}, u32[]{:S(2)}, u32[]{:S(2)}) async-start(bf16[16,96,128]{2,1,0:T(8,128)(2,1)} %get-tuple-element.44), calls=%async_computation | async-start | bytes 786432 | tf_op jit(solution)/shard_map/all_to_all | solution.py:70
  42.0 38.2 %copy-start.5 = (bf16[6,96,128]{2,1,0:T(8,128)(2,1)S(1)}, bf16[6,96,128]{2,1,0:T(8,128)(2,1)}, u32[]{:S(2)}) copy-start(bf16[6,96,128]{2,1,0:T(8,128)(2,1)} %seed_ref.1) | copy-start | bytes 442372
  68.4 38.1 %copy-start.6 = (bf16[128,128]{1,0:T(8,128)(2,1)S(1)}, bf16[128,128]{1,0:T(8,128)(2,1)}, u32[]{:S(2)}) copy-start(bf16[128,128]{1,0:T(8,128)(2,1)} %final_out_ref.1) | copy-start | bytes 98308
  144.8 18.2 %copy-start.3 = (bf16[64,6,256]{2,0,1:T(8,128)(2,1)S(1)}, bf16[64,6,256]{2,0,1:T(8,128)(2,1)}, u32[]{:S(2)}) copy-start(bf16[64,6,256]{2,0,1:T(8,128)(2,1)} %param.10) | copy-start | bytes 589828
  144.8 18.2 %copy-start.9 = (bf16[256,64]{0,1:T(8,128)(2,1)S(1)}, bf16[256,64]{0,1:T(8,128)(2,1)}, u32[]{:S(2)}) copy-start(bf16[256,64]{0,1:T(8,128)(2,1)} %param.11) | copy-start | bytes 98308

commit v4 on v2

--- a/solution.py
+++ b/solution.py
@@ -407,22 +407,25 @@
     return lax.dot_general(a, b, (((0,), (0,)), ((), ())), preferred_element_type=F32)
 
 
-def launch(body, outs, args, scratch=(), name=None, flops=2e8):
+def launch(body, outs, args, scratch=(), name=None, flops=2e8, raw=False):
     vmem = pl.BlockSpec(memory_space=pltpu.VMEM)
+    held = pl.BlockSpec(memory_space=pltpu.HBM) if raw else vmem
+    if raw:
+        args = [pltpu.with_memory_space_constraint(a, pltpu.HBM) for a in args]
     moved = sum(a.size * a.dtype.itemsize for a in args) + sum(
         o.size * o.dtype.itemsize for o in outs
     )
     return pl.pallas_call(
         body,
         out_shape=outs,
-        in_specs=[vmem] * len(args),
+        in_specs=[held] * len(args),
         out_specs=[vmem] * len(outs),
         scratch_shapes=list(scratch),
         name=name,
         cost_estimate=pl.CostEstimate(
             flops=int(flops), bytes_accessed=int(moved), transcendentals=0
         ),
-        compiler_params=pltpu.CompilerParams(vmem_limit_bytes=40 * 1024 * 1024),
+        compiler_params=pltpu.CompilerParams(vmem_limit_bytes=24 * 1024 * 1024),
     )(*args)
 
 
@@ -442,6 +445,8 @@
 
 
 def tall(x):
+    if x.shape[0] == LANES:
+        return x
     return jnp.concatenate([x, jnp.zeros((LANES - x.shape[0], x.shape[1]), x.dtype)], axis=0)
 
 
@@ -455,22 +460,141 @@
     return left, right
 
 
-def send_pair(out_ref, row, left, right, groups):
-    both = jnp.concatenate([dealt(left, groups), dealt(right, groups)], axis=1)
-    wide = both.shape[1]
-    out_ref[:, row * wide : (row + 1) * wide, :] = both.astype(BF16)
-
-
-def msa_kernel(sizes, msa_ref, flank_t_ref, send_ref, normal_ref, left_ref):
+def lanes_of(x):
+    return lax.broadcasted_iota(jnp.int32, x.shape, x.ndim - 1)
+
+
+def shifted(x, amount):
+    amount = amount % LANES
+    return x if amount == 0 else pltpu.roll(x, amount, x.ndim - 1)
+
+
+def split_rows(tiles, rows, residues):
+    out = []
+    lane = lanes_of(tiles[0])
+    for row in range(rows):
+        tile, offset = divmod(row * residues, LANES)
+        piece = shifted(tiles[tile], -offset)
+        if offset + residues > LANES:
+            piece = jnp.where(lane < LANES - offset, piece, shifted(tiles[tile + 1], -offset))
+        out.append(jnp.where(lane < residues, piece, 0.0))
+    return out
+
+
+def join_rows(values, residues, count):
+    out = [None] * count
+    lane = lanes_of(values[0])
+    for row, value in enumerate(values):
+        tile, offset = divmod(row * residues, LANES)
+        moved = shifted(value, offset)
+        out[tile] = moved if out[tile] is None else jnp.where(lane >= offset, moved, out[tile])
+        if offset + residues > LANES:
+            out[tile + 1] = jnp.where(lane < offset + residues - LANES, moved, 0.0)
+    return out
+
+
+class Layout:
+    def __init__(self, rows, residues, share):
+        self.rows, self.residues, self.share = rows, residues, share
+        self.cells = rows * residues
+        self.tiles = -(-self.cells // LANES)
+        self.spots = self.tiles * LANES
+        rest = self.cells % LANES
+        self.paired = 0 < rest <= LANES // 2
+        self.single = self.tiles * share
+        self.double = self.tiles * 2 * share - (share if self.paired else 0)
+
+    def shared(self, tile):
+        return self.paired and tile == self.tiles - 1
+
+    def lanes(self, tile):
+        return slice(tile * LANES, (tile + 1) * LANES)
+
+    def filled(self, tile):
+        return min(LANES, self.cells - tile * LANES)
+
+    def pack(self, out_ref, tile, left, right):
+        start = tile * 2 * self.share
+        if self.shared(tile):
+            both = jnp.where(lanes_of(left) < LANES // 2, left, shifted(right, LANES // 2))
+        else:
+            both = jnp.concatenate([left, right], axis=1)
+        out_ref[:, start : start + both.shape[1], :] = both.astype(BF16)
+
+    def unpack(self, both_ref, tile):
+        start = tile * 2 * self.share
+        left = both_ref[:, start : start + self.share, :].astype(F32)
+        if self.shared(tile):
+            low = lanes_of(left) < LANES // 2
+            right = jnp.where(low, shifted(left, LANES // 2), 0.0)
+            return jnp.where(low, left, 0.0), right
+        start += self.share
+        return left, both_ref[:, start : start + self.share, :].astype(F32)
+
+    def spread_pairs(self, both_ref, wide_ref):
+        tiles = [
+            jnp.concatenate(self.unpack(both_ref, tile), axis=1) for tile in range(self.tiles)
+        ]
+        self.spread(tiles, wide_ref)
+
+    def spread_singles(self, grad_ref, wide_ref):
+        tiles = [
+            grad_ref[:, tile * self.share : (tile + 1) * self.share, :].astype(F32)
+            for tile in range(self.tiles)
+        ]
+        self.spread(tiles, wide_ref)
+
+    def spread(self, tiles, wide_ref):
+        wide = tiles[0].shape[1]
+        for row, value in enumerate(split_rows(tiles, self.rows, self.residues)):
+            for group in range(value.shape[0]):
+                at = (group * self.rows + row) * wide
+                wide_ref[at : at + wide, :] = value[group]
+
+    def collect(self, result_ref, groups):
+        wide = result_ref.shape[0] // (groups * self.rows)
+        whole = result_ref[...].reshape(groups, self.rows * wide, LANES)
+        values = [whole[:, row * wide : (row + 1) * wide, :] for row in range(self.rows)]
+        return join_rows(values, self.residues, self.tiles)
+
+
+def turned(to_ref, from_ref):
+    for tile in range(from_ref.shape[1] // LANES):
+        lanes = slice(tile * LANES, (tile + 1) * LANES)
+        to_ref[lanes, :] = from_ref[:, lanes].astype(F32).T.astype(BF16)
+
+
+def msa_kernel(sizes, *refs):
     rows, depth, hidden, groups = sizes
+    sources, refs = refs[:7], refs[7:]
+    (
+        send_ref,
+        normal_ref,
+        left_ref,
+        sorted_ref,
+        sorted_t_ref,
+        gates_out_t_ref,
+        gates_in_t_ref,
+        final_out_t_ref,
+        final_in_t_ref,
+    ) = refs[:9]
+    held, wide_ref, semaphores = refs[9:16], refs[16], refs[17]
+    copies = [
+        pltpu.make_async_copy(source, target, semaphores.at[at])
+        for at, (source, target) in enumerate(zip(sources, held))
+    ]
+    for copy in copies:
+        copy.start()
+    msa_ref, flank_t_ref, final_ref, gates_out_ref, gates_in_ref, final_out_ref, final_in_ref = held
+    copies[0].wait()
+    copies[1].wait()
     for row in range(rows):
         hatted, _ = moments(msa_ref[row].astype(F32), 1)
         normal = hatted.astype(BF16)
         normal_ref[row] = normal
         twice = jnp.concatenate([normal, normal], axis=0)
         mapped = nt(flank_t_ref[...], twice)
-        lane = lax.broadcasted_iota(jnp.int32, (hidden, LANES), 1)
-        low = lane < depth
+        low = lax.broadcasted_iota(jnp.int32, (hidden, LANES), 1) < depth
         left = mapped[:hidden]
         left_ref[row * hidden : (row + 1) * hidden] = jnp.where(low, left, 0.0).astype(BF16)
         left_ref[(rows + row) * hidden : (rows + row + 1) * hidden] = jnp.where(
@@ -482,6 +606,20 @@
         ).astype(BF16)
         for group in range(groups):
             send_ref[group, row * half : (row + 1) * half, :] = right
+    for copy in copies[2:]:
+        copy.wait()
+    wide_ref[...] = final_ref[...].astype(F32)
+    for d in range(hidden):
+        sorted_ref[d * hidden : (d + 1) * hidden, :] = wide_ref[
+            pl.ds(d, hidden, stride=hidden), :
+        ].astype(BF16)
+    for tile in range(hidden * hidden // LANES):
+        at = slice(tile * LANES, (tile + 1) * LANES)
+        sorted_t_ref[:, at] = sorted_ref[at, :].astype(F32).T.astype(BF16)
+    turned(gates_out_t_ref, gates_out_ref)
+    turned(gates_in_t_ref, gates_in_ref)
+    turned(final_out_t_ref, final_out_ref)
+    turned(final_in_t_ref, final_in_ref)
 
 
 def outer_kernel(
@@ -497,7 +635,8 @@
     pair_ref,
     wide_ref,
 ):
-    rows, residues, depth, hidden, groups, width = sizes
+    layout, depth, hidden, groups, width = sizes
+    rows, residues = layout.rows, layout.residues
     half = hidden // 2
     wide_ref[...] = right_ref[...].reshape(wide_ref.shape).astype(F32)
     for d in range(half):
@@ -514,20 +653,25 @@
                         at : at + hidden, e * LANES : (e + 1) * LANES
                     ].astype(BF16)
     update = nn(final_t_ref[...], outer_ref[...])
-    for row in range(rows):
-        lanes = slice(row * LANES, (row + 1) * LANES)
-        entry = tall(edge_ref[row].astype(F32)).T
-        pair = (entry + update[:, lanes]).astype(BF16)
+    update = join_rows(
+        [update[:, row * LANES : (row + 1) * LANES] for row in range(rows)], residues, layout.tiles
+    )
+    for tile in range(layout.tiles):
+        lanes = layout.lanes(tile)
+        at = tile * LANES
+        entry = tall(edge_ref[at : at + layout.filled(tile), :].astype(F32)).T
+        pair = (entry + update[tile]).astype(BF16)
         pair_ref[:, lanes] = pair
         hatted, _ = moments(pair.astype(F32), 0)
         projected = nn(gates_t_ref[: 4 * width, :], hatted.astype(BF16))
         left, right = gated_pair(projected, width)
-        send_pair(send_ref, row, left, right, groups)
+        layout.pack(send_ref, tile, dealt(left, groups), dealt(right, groups))
 
 
 def triangle_kernel(sizes, outgoing, both_ref, send_ref, wide_ref, result_ref):
-    residues, share = sizes
-    wide_ref[...] = both_ref[...].reshape(wide_ref.shape).astype(F32)
+    layout, groups = sizes
+    residues, share = layout.residues, layout.share
+    layout.spread_pairs(both_ref, wide_ref)
     for c in range(share):
         left = wide_ref[pl.ds(c, residues, stride=2 * share), :].astype(BF16)
         right = wide_ref[pl.ds(share + c, residues, stride=2 * share), :].astype(BF16)
@@ -536,16 +680,17 @@
         else:
             product = tn(left, right)[:residues]
         result_ref[pl.ds(c, residues, stride=share), :] = product
-    send_ref[...] = result_ref[...].astype(BF16).reshape(send_ref.shape)
+    for tile, value in enumerate(layout.collect(result_ref, groups)):
+        send_ref[:, tile * share : (tile + 1) * share, :] = value.astype(BF16)
 
 
 def triangle_adjoint_kernel(
     sizes, outgoing, both_ref, grad_ref, send_ref, wide_ref, tri_ref, result_ref
 ):
-    residues, share, rows, riders = sizes
-    own = rows * share
-    wide_ref[...] = both_ref[...].reshape(wide_ref.shape).astype(F32)
-    tri_ref[...] = grad_ref[:, :own, :].astype(F32).reshape(tri_ref.shape)
+    layout, groups, riders = sizes
+    residues, share = layout.residues, layout.share
+    layout.spread_pairs(both_ref, wide_ref)
+    layout.spread_singles(grad_ref, tri_ref)
     for c in range(share):
         left = wide_ref[pl.ds(c, residues, stride=2 * share), :].astype(BF16)
         right = wide_ref[pl.ds(share + c, residues, stride=2 * share), :].astype(BF16)
@@ -558,14 +703,17 @@
             grad_right = nn(left, tall(grad))
         result_ref[pl.ds(c, residues, stride=2 * share), :] = grad_left
         result_ref[pl.ds(share + c, residues, stride=2 * share), :] = grad_right
-    groups = send_ref.shape[0]
-    send_ref[:, : 2 * own, :] = (
-        result_ref[...].astype(BF16).reshape(groups, 2 * own, LANES)
-    )
+    for tile, value in enumerate(layout.collect(result_ref, groups)):
+        layout.pack(send_ref, tile, value[:, :share, :], value[:, share:, :])
     if riders:
-        summed = jnp.sum(grad_ref[:, own:, :].astype(F32), axis=0).astype(BF16)
+        summed = jnp.sum(grad_ref[:, layout.single :, :].astype(F32), axis=0).astype(BF16)
         for group in range(groups):
-            send_ref[group, 2 * own :, :] = summed
+            send_ref[group, layout.double :, :] = summed
+
+
+def tri_tile(layout, tri_ref, tile, width):
+    share = layout.share
+    return tri_ref[:, tile * share : (tile + 1) * share, :].astype(F32).reshape(width, LANES)
 
 
 def middle_kernel(
@@ -578,12 +726,10 @@
     send_ref,
     next_ref,
 ):
-    rows, groups, width = sizes
-    share = width // groups
-    received = tri_ref[...].astype(F32)
-    for row in range(rows):
-        lanes = slice(row * LANES, (row + 1) * LANES)
-        tri = received[:, row * share : (row + 1) * share, :].reshape(width, LANES)
+    layout, groups, width = sizes
+    for tile in range(layout.tiles):
+        lanes = layout.lanes(tile)
+        tri = tri_tile(layout, tri_ref, tile, width)
         unit, _ = moments(tri, 0)
         values = nn(final_t_ref[...], unit.astype(BF16))
         pair = pair_ref[:, lanes].astype(F32)
@@ -594,7 +740,7 @@
         hatted, _ = moments(following.astype(F32), 0)
         projected = nn(next_gates_t_ref[: 4 * width, :], hatted.astype(BF16))
         left, right = gated_pair(projected, width)
-        send_pair(send_ref, row, left, right, groups)
+        layout.pack(send_ref, tile, dealt(left, groups), dealt(right, groups))
 
 
 def tri_adjoint_row(tri, pair, gradient, gates_t_ref, final_ref, final_t_ref, width):
@@ -627,14 +773,15 @@
     unit_ref,
     scaled_ref,
 ):
-    rows, residues, groups, width = sizes
-    share = width // groups
-    received = tri_ref[...].astype(F32)
-    for row in range(rows):
-        lanes = slice(row * LANES, (row + 1) * LANES)
-        tri = received[:, row * share : (row + 1) * share, :].reshape(width, LANES)
+    layout, groups, width = sizes
+    share = layout.share
+    for tile in range(layout.tiles):
+        lanes = layout.lanes(tile)
+        at = tile * LANES
+        filled = layout.filled(tile)
+        tri = tri_tile(layout, tri_ref, tile, width)
         pair = pair_ref[:, lanes].astype(F32)
-        gradient = tall(seed_ref[row].astype(F32)).T
+        gradient = tall(seed_ref[at : at + filled, :].astype(F32)).T
         seed_t_ref[:, lanes] = gradient.astype(BF16)
         unit, scaled, values, gate, grad_tri, grad_gate = tri_adjoint_row(
             tri, pair, gradient, gates_t_ref, final_ref, final_t_ref, width
@@ -642,17 +789,19 @@
         unit_ref[:, lanes] = unit
         scaled_ref[:, lanes] = scaled
         grad_gate_ref[:, lanes] = grad_gate
-        grads_ref[:, row * share : (row + 1) * share, :] = dealt(grad_tri, groups)
-        out_ref[row] = (pair + gate * values).T[:residues].astype(BF16)
+        grads_ref[:, tile * share : (tile + 1) * share, :] = dealt(grad_tri, groups)
+        out_ref[at : at + filled, :] = (pair + gate * values).T[:filled].astype(BF16)
     send_ref[...] = grads_ref[...].astype(BF16)
     final_sum_ref[...] = nt(unit_ref[...], scaled_ref[...])
 
 
-def proj_adjoint_row(row, received, pair, grad_gate, gates_t_ref, gates_ref, normal_ref, proj_ref, width):
-    share2 = received.shape[1]
-    lanes = slice(row * LANES, (row + 1) * LANES)
-    grad_left = received[:, : share2 // 2, :].reshape(width, LANES)
-    grad_right = received[:, share2 // 2 :, :].reshape(width, LANES)
+def proj_adjoint_row(
+    layout, tile, both_ref, pair, grad_gate, gates_t_ref, gates_ref, normal_ref, proj_ref, width
+):
+    lanes = layout.lanes(tile)
+    grad_left, grad_right = layout.unpack(both_ref, tile)
+    grad_left = grad_left.reshape(width, LANES)
+    grad_right = grad_right.reshape(width, LANES)
     hatted, factor = moments(pair, 0)
     normal = hatted.astype(BF16)
     normal_ref[:, lanes] = normal
@@ -705,16 +854,15 @@
     unit_ref,
     scaled_ref,
 ):
-    rows, groups, width = sizes
-    share = width // groups
-    received = tri_ref[...].astype(F32)
-    for row in range(rows):
-        lanes = slice(row * LANES, (row + 1) * LANES)
+    layout, groups, width = sizes
+    share = layout.share
+    for tile in range(layout.tiles):
+        lanes = layout.lanes(tile)
         pair = pair_in_ref[:, lanes].astype(F32)
-        both = both_ref[:, row * 2 * share : (row + 1) * 2 * share, :].astype(F32)
         gradient = seed_ref[:, lanes].astype(F32) + proj_adjoint_row(
-            row,
-            both,
+            layout,
+            tile,
+            both_ref,
             pair,
             grad_gate_in_ref[:, lanes],
             gates_in_t_ref,
@@ -724,7 +872,7 @@
             width,
         )
         grad_ref[:, lanes] = gradient
-        tri = received[:, row * share : (row + 1) * share, :].reshape(width, LANES)
+        tri = tri_tile(layout, tri_ref, tile, width)
         unit, scaled, _, _, grad_tri, grad_gate = tri_adjoint_row(
             tri,
             pair_out_ref[:, lanes].astype(F32),
@@ -737,8 +885,8 @@
         unit_ref[:, lanes] = unit
         scaled_ref[:, lanes] = scaled
         grad_gate_ref[:, lanes] = grad_gate
-        grads_ref[:, row * share : (row + 1) * share, :] = dealt(grad_tri, groups)
-    place = rows * share
+        grads_ref[:, tile * share : (tile + 1) * share, :] = dealt(grad_tri, groups)
+    place = layout.single
     place = deal_rows(grads_ref, place, nt(normal_ref[...], proj_ref[...]), groups)
     place = deal_rows(grads_ref, place, final_in_sum_ref[...], groups)
     deal_rows(grads_ref, place, nt(unit_ref[...], scaled_ref[...]), groups)
@@ -769,9 +917,6 @@
     send_ref,
     adjoint_ref,
     left_grad_ref,
-    proj_in_ref,
-    final_in_ref,
-    final_out_ref,
     grads_ref,
     normal_ref,
     proj_ref,
@@ -779,15 +924,16 @@
     outer_grad_ref,
     right_grad_ref,
 ):
-    rows, residues, depth, hidden, groups, width = sizes
-    share = width // groups
+    layout, depth, hidden, groups, width = sizes
+    rows, residues = layout.rows, layout.residues
     half = hidden // 2
-    for row in range(rows):
-        lanes = slice(row * LANES, (row + 1) * LANES)
-        both = both_ref[:, row * 2 * share : (row + 1) * 2 * share, :].astype(F32)
+    adjoints = []
+    for tile in range(layout.tiles):
+        lanes = layout.lanes(tile)
         gradient = grad_ref[:, lanes] + proj_adjoint_row(
-            row,
-            both,
+            layout,
+            tile,
+            both_ref,
             pair_ref[:, lanes].astype(F32),
             grad_gate_ref[:, lanes],
             gates_t_ref,
@@ -796,9 +942,14 @@
             proj_ref,
             width,
         )
-        adjoint = gradient.astype(BF16)
-        adjoint_t_ref[:, lanes] = adjoint
-        adjoint_ref[row] = adjoint.astype(F32).T[:residues].astype(BF16)
+        adjoint = gradient.astype(BF16).astype(F32)
+        adjoints.append(adjoint)
+        at = tile * LANES
+        filled = layout.filled(tile)
+        adjoint_ref[at : at + filled, :] = adjoint.T[:filled].astype(BF16)
+    for row, value in enumerate(split_rows(adjoints, rows, residues)):
+        adjoint = value.astype(BF16)
+        adjoint_t_ref[:, row * LANES : (row + 1) * LANES] = adjoint
         spread_grad = nn(final_ref[...], adjoint).astype(BF16)
         for h in range(2):
             for d in range(half):
@@ -834,14 +985,6 @@
     used = (flank.shape[1] // LANES) * (hidden // SUB)
     grads_ref[used:, place : place + SUB, :] = jnp.zeros((groups - used, SUB, LANES), F32)
     send_ref[...] = grads_ref[...].astype(BF16)
-    rest = both_ref[:, rows * 2 * share :, :].astype(F32)
-    tiles, place = gathered_rows(rest, 0, proj_in_ref.shape[1] // LANES, width)
-    for tile, value in enumerate(tiles):
-        proj_in_ref[:, tile * LANES : (tile + 1) * LANES] = value / residues
-    tiles, place = gathered_rows(rest, place, 1, width)
-    final_in_ref[...] = tiles[0] / residues
-    tiles, place = gathered_rows(rest, place, 1, width)
-    final_out_ref[...] = tiles[0] / residues
 
 
 def msa_adjoint_kernel(
@@ -880,8 +1023,33 @@
             send_ref[group, at : at + hidden, :] = flank[:, tile * LANES : (tile + 1) * LANES]
 
 
-def totals_kernel(sizes, parts_ref, proj_ref, final_ref, flank_ref, wide_ref):
-    residues, hidden, groups, width = sizes
+def totals_kernel(
+    sizes,
+    parts_ref,
+    both_ref,
+    updated_ref,
+    adjoint_ref,
+    proj_ref,
+    final_ref,
+    flank_ref,
+    proj_in_ref,
+    final_in_ref,
+    final_out_ref,
+    updated_out_ref,
+    adjoint_out_ref,
+    wide_ref,
+):
+    layout, hidden, groups, width = sizes
+    residues = layout.residues
+    updated_out_ref[...] = updated_ref[...]
+    adjoint_out_ref[...] = adjoint_ref[...]
+    rest = both_ref[:, layout.double :, :].astype(F32)
+    tiles, place = gathered_rows(rest, 0, proj_in_ref.shape[1] // LANES, width)
+    for tile, value in enumerate(tiles):
+        proj_in_ref[:, tile * LANES : (tile + 1) * LANES] = value / residues
+    for target_ref in (final_in_ref, final_out_ref):
+        tiles, place = gathered_rows(rest, place, 1, width)
+        target_ref[...] = tiles[0] / residues
     parts = parts_ref[...].astype(F32)
     tiles, place = gathered_rows(parts, 0, proj_ref.shape[1] // LANES, width)
     for tile, value in enumerate(tiles):
@@ -917,7 +1085,8 @@
     hidden = tensor_flank_matrix.shape[1] // 2
     half = hidden // 2
     share = width // groups
-    spots = rows * LANES
+    layout = Layout(rows, residues, share)
+    spots = layout.spots
     square = hidden * hidden
 
     def shape(*dims, dtype=BF16):
@@ -925,44 +1094,71 @@
 
     msa = jnp.swapaxes(alignment_embedding, 0, 1)
     flank_t = tensor_flank_matrix.T
-    send, msa_normal, left = launch(
+    (
+        send,
+        msa_normal,
+        left,
+        final_sorted,
+        final_sorted_t,
+        gates_out_t,
+        gates_in_t,
+        final_out_t,
+        final_in_t,
+    ) = launch(
         partial(msa_kernel, (rows, depth, hidden, groups)),
         [
             shape(groups, rows * half, LANES),
             shape(rows, depth, features),
             shape(2 * rows * hidden, LANES),
+            shape(square, width),
+            shape(width, square),
+            shape(5 * width, width),
+            shape(5 * width, width),
+            shape(width, width),
+            shape(width, width),
         ],
-        (msa, flank_t),
+        (
+            msa,
+            flank_t,
+            tensor_final_matrix,
+            outward_sigmoid_matrix,
+            inward_sigmoid_matrix,
+            outward_final_matrix,
+            inward_final_matrix,
+        ),
+        [
+            pltpu.VMEM((rows, depth, features), BF16),
+            pltpu.VMEM((2 * hidden, features), BF16),
+            pltpu.VMEM((square, width), BF16),
+            pltpu.VMEM((width, 5 * width), BF16),
+            pltpu.VMEM((width, 5 * width), BF16),
+            pltpu.VMEM((width, width), BF16),
+            pltpu.VMEM((width, width), BF16),
+            pltpu.VMEM((square, width), F32),
+            pltpu.SemaphoreType.DMA((7,)),
+        ],
         name="msa",
+        raw=True,
     )
     right = exchanged(send)
 
-    final_sorted = (
-        tensor_final_matrix.reshape(hidden, hidden, width).swapaxes(0, 1).reshape(square, width)
-    )
-    final_sorted_t = final_sorted.T
-    gates_out_t = outward_sigmoid_matrix.T
-    gates_in_t = inward_sigmoid_matrix.T
-    final_out_t = outward_final_matrix.T
-    final_in_t = inward_final_matrix.T
-
     send, spread, outer, pair_one = launch(
-        partial(outer_kernel, (rows, residues, depth, hidden, groups, width)),
+        partial(outer_kernel, (layout, depth, hidden, groups, width)),
         [
-            shape(groups, rows * 2 * share, LANES),
+            shape(groups, layout.double, LANES),
             shape(half * LANES, LANES),
-            shape(square, spots),
+            shape(square, rows * LANES),
             shape(width, spots),
         ],
-        (right, left, edge_embedding, final_sorted_t, gates_out_t),
+        (right, left, edge_embedding.reshape(-1, width), final_sorted_t, gates_out_t),
         [pltpu.VMEM((residues * half, LANES), F32)],
         name="outer",
     )
 
     def triangle(both, outgoing):
         return launch(
-            partial(triangle_kernel, (residues, share), outgoing),
-            [shape(groups, rows * share, LANES)],
+            partial(triangle_kernel, (layout, groups), outgoing),
+            [shape(groups, layout.single, LANES)],
             (both,),
             [
                 pltpu.VMEM((residues * 2 * share, LANES), F32),
@@ -972,10 +1168,10 @@
         )[0]
 
     def triangle_adjoint(both, grads, outgoing):
-        riders = grads.shape[1] - rows * share
+        riders = grads.shape[1] - layout.single
         return launch(
-            partial(triangle_adjoint_kernel, (residues, share, rows, riders), outgoing),
-            [shape(groups, rows * 2 * share + riders, LANES)],
+            partial(triangle_adjoint_kernel, (layout, groups, riders), outgoing),
+            [shape(groups, layout.double + riders, LANES)],
             (both, grads),
             [
                 pltpu.VMEM((residues * 2 * share, LANES), F32),
@@ -988,25 +1184,25 @@
     both_out = exchanged(send)
     tri_out = exchanged(triangle(both_out, True))
     send, pair_two = launch(
-        partial(middle_kernel, (rows, groups, width)),
-        [shape(groups, rows * 2 * share, LANES), shape(width, spots)],
+        partial(middle_kernel, (layout, groups, width)),
+        [shape(groups, layout.double, LANES), shape(width, spots)],
         (tri_out, pair_one, gates_out_t, final_out_t, gates_in_t),
         name="middle",
     )
     both_in = exchanged(send)
     tri_in = exchanged(triangle(both_in, False))
     send, updated, seed_t, grad_gate_in, final_in_sum = launch(
-        partial(turn_kernel, (rows, residues, groups, width)),
+        partial(turn_kernel, (layout, groups, width)),
         [
-            shape(groups, rows * share, LANES),
-            shape(rows, residues, width),
+            shape(groups, layout.single, LANES),
+            shape(rows * residues, width),
             shape(width, spots),
             shape(width, spots),
             shape(width, width, dtype=F32),
         ],
-        (tri_in, pair_two, adjoint_seed, gates_in_t, inward_final_matrix, final_in_t),
+        (tri_in, pair_two, adjoint_seed.reshape(-1, width), gates_in_t, inward_final_matrix, final_in_t),
         [
-            pltpu.VMEM((groups, rows * share, LANES), F32),
+            pltpu.VMEM((groups, layout.single, LANES), F32),
             pltpu.VMEM((width, spots), BF16),
             pltpu.VMEM((width, spots), BF16),
         ],
@@ -1015,9 +1211,9 @@
     grads = exchanged(triangle_adjoint(both_in, exchanged(send), False))
     riders = share * (gates_in_t.shape[0] // LANES + 2)
     send, grad_two, grad_gate_out = launch(
-        partial(between_kernel, (rows, groups, width)),
+        partial(between_kernel, (layout, groups, width)),
         [
-            shape(groups, rows * share + riders, LANES),
+            shape(groups, layout.single + riders, LANES),
             shape(width, spots, dtype=F32),
             shape(width, spots),
         ],
@@ -1036,7 +1232,7 @@
             final_out_t,
         ),
         [
-            pltpu.VMEM((groups, rows * share + riders, LANES), F32),
+            pltpu.VMEM((groups, layout.single + riders, LANES), F32),
             pltpu.VMEM((width, spots), BF16),
             pltpu.VMEM((5 * width, spots), BF16),
             pltpu.VMEM((width, spots), BF16),
@@ -1046,15 +1242,12 @@
     )
     grads = exchanged(triangle_adjoint(both_out, exchanged(send), True))
     count = rows * half + share * 5 + square // groups + SUB
-    send, edge_adjoint, left_grad, proj_in, final_in, final_out = launch(
-        partial(close_kernel, (rows, residues, depth, hidden, groups, width)),
+    send, edge_adjoint, left_grad = launch(
+        partial(close_kernel, (layout, depth, hidden, groups, width)),
         [
             shape(groups, count, LANES),
-            shape(rows, residues, width),
+            shape(rows * residues, width),
             shape(rows * hidden, LANES),
-            shape(width, 5 * width, dtype=F32),
-            shape(width, width, dtype=F32),
-            shape(width, width, dtype=F32),
         ],
         (
             grads,
@@ -1073,7 +1266,7 @@
             pltpu.VMEM((groups, count, LANES), F32),
             pltpu.VMEM((width, spots), BF16),
             pltpu.VMEM((5 * width, spots), BF16),
-            pltpu.VMEM((width, spots), BF16),
+            pltpu.VMEM((width, rows * LANES), BF16),
             pltpu.VMEM((2 * rows * hidden, half * LANES), BF16),
             pltpu.VMEM((residues * half, LANES), F32),
         ],
@@ -1089,20 +1282,25 @@
         (exchanged(send), left_grad, msa, msa_normal, flank_t),
         name="msa_adjoint",
     )
-    proj_out, outer_final, outer_proj_t = launch(
-        partial(totals_kernel, (residues, hidden, groups, width)),
+    proj_out, outer_final, outer_proj_t, proj_in, final_in, final_out, updated, edge_adjoint = launch(
+        partial(totals_kernel, (layout, hidden, groups, width)),
         [
             shape(width, 5 * width, dtype=F32),
             shape(square, width, dtype=F32),
             shape(2 * hidden, features, dtype=F32),
+            shape(width, 5 * width, dtype=F32),
+            shape(width, width, dtype=F32),
+            shape(width, width, dtype=F32),
+            shape(rows * residues, width),
+            shape(rows * residues, width),
         ],
-        (exchanged(send),),
+        (exchanged(send), grads, updated, edge_adjoint),
         [pltpu.VMEM((square, width), F32)],
         name="totals",
     )
     return (
-        updated,
-        edge_adjoint,
+        updated.reshape(edge_embedding.shape),
+        edge_adjoint.reshape(edge_embedding.shape),
         jnp.swapaxes(msa_adjoint, 0, 1),
         outer_proj_t.T,
         outer_final,

time: 195 us -> 181 us (0.928)
  blocking collectives: 121 us -> 161 us
  waiting for transfers between devices: 26.5 us -> 0 us
  starting transfers between devices: 16.1 us -> 0 us
  local copies, waits for them, and re-layouts: 9.44 us -> 0.04 us
  Pallas kernels: 19.8 us -> 17.8 us
    all_to_all x8 -> x11, blocking collectives: 121 us -> 161 us  [exchanged(): lax.all_to_all(values, 'dap', split_axis=0, concat_axis=0, tiled=True)]
    all_to_all x3 -> x0, waiting for transfers between devices: 26.5 us -> none  [exchanged(): lax.all_to_all(values, 'dap', split_axis=0, concat_axis=0, tiled=True)]
    all_to_all x3 -> x0, starting transfers between devices: 16.1 us -> none  [exchanged(): lax.all_to_all(values, 'dap', split_axis=0, concat_axis=0, tiled=True)]
    unnamed x54 -> x16, local copies, waits for them, and re-layouts: 9.19 us -> 0.04 us
    pallas_call x12, Pallas kernels: 19.8 us -> 17.8 us  [launch(): pl.pallas_call(body, out_shape=outs, in_specs=[held] * len(args), out_spe...]
  transfers between devices with their start and end apart: 3 -> 0, of which waited for: 3 -> 0; matrix products, arithmetic and copies ran while one was open for 1% -> 0% of each run, Pallas kernels for 0% -> 0%
where the time goes in v4:
time: 181 us; the launch traced here: 180 us
  blocking collectives  161 us (89%)
  Pallas kernels  17.8 us (10%)
    all_to_all x11, blocking collectives, exchanged(): lax.all_to_all(values, 'dap', split_axis=0, concat_axis=0, tiled=True)  161 us
    pallas_call x12, Pallas kernels, launch(): pl.pallas_call(body, out_shape=outs, in_specs=[held] * len(args), out_spe...  17.8 us

profile of v4, /device:TPU:0, one launch (start us, length us, event | category | flops | bytes accessed | tf_op | source)
XLA Modules:
  0.0 180.0 jit_solution(7383770460106932530)
XLA Ops:
  0.7 2.0 %msa.1 = (bf16[16,96,128]{2,1,0:T(8,128)(2,1)S(1)}, bf16[6,64,256]{2,1,0:T(8,128)(2,1)S(1)}, bf16[384,128]{1,0:T(8,128)(2,1)S(1)}, bf16[1024,128]{1,0:T(8,128)(2...) custom-call(bf16[6,64,256]{2,1,0:T(8,128)(2,1)} %bitcast.8, ...), custom_call_target="tpu_custom_call" | custom-call | flops 200000000 | bytes 2490368 | tf_op jit(solution)/shard_map/msa/pallas_call | solution.py:418
  2.7 20.8 %all_to_all.55.right_ref = bf16[16,96,128]{2,1,0:T(8,128)(2,1)S(1)} all-to-all(bf16[16,96,128]{2,1,0:T(8,128)(2,1)S(1)} %get-tuple-element.45), channel_id=1, replica_groups=mesh['dap'=16,'dp'=2] {'dap'}, dimensions={0} | all-to-all | bytes 786432 | tf_op jit(solution)/shard_map/all_to_all | solution.py:70
  23.4 1.5 outer.1
  25.0 13.5 %all_to_all.56.both_ref = bf16[16,72,128]{2,1,0:T(8,128)(2,1)S(1)} all-to-all(bf16[16,72,128]{2,1,0:T(8,128)(2,1)S(1)} %get-tuple-element.49), channel_id=1, replica_groups=mesh['dap'=16,'dp'=2] {'dap'}, dimensions={0} | all-to-all | bytes 589824 | tf_op jit(solution)/shard_map/all_to_all | solution.py:70
  38.5 0.6 triangle_out.1
  39.1 11.2 %all_to_all.57.tri_ref = bf16[16,40,128]{2,1,0:T(8,128)(2,1)S(1)} all-to-all(bf16[16,40,128]{2,1,0:T(8,128)(2,1)S(1)} %triangle_out.1), channel_id=1, replica_groups=mesh['dap'=16,'dp'=2] {'dap'}, dimensions={0} | all-to-all | bytes 327680 | tf_op jit(solution)/shard_map/all_to_all | solution.py:70
  50.3 1.2 middle.1
  51.5 11.6 %all_to_all.58.both_ref = bf16[16,72,128]{2,1,0:T(8,128)(2,1)S(1)} all-to-all(bf16[16,72,128]{2,1,0:T(8,128)(2,1)S(1)} %get-tuple-element.53), channel_id=1, replica_groups=mesh['dap'=16,'dp'=2] {'dap'}, dimensions={0} | all-to-all | bytes 589824 | tf_op jit(solution)/shard_map/all_to_all | solution.py:70
  63.0 0.6 triangle_in.1
  63.7 11.4 %all_to_all.59.tri_ref = bf16[16,40,128]{2,1,0:T(8,128)(2,1)S(1)} all-to-all(bf16[16,40,128]{2,1,0:T(8,128)(2,1)S(1)} %triangle_in.1), channel_id=1, replica_groups=mesh['dap'=16,'dp'=2] {'dap'}, dimensions={0} | all-to-all | bytes 327680 | tf_op jit(solution)/shard_map/all_to_all | solution.py:70
  75.0 1.1 turn.1
  76.2 10.8 %all_to_all.60.grad_ref = bf16[16,40,128]{2,1,0:T(8,128)(2,1)S(1)} all-to-all(bf16[16,40,128]{2,1,0:T(8,128)(2,1)S(1)} %get-tuple-element.56), channel_id=1, replica_groups=mesh['dap'=16,'dp'=2] {'dap'}, dimensions={0} | all-to-all | bytes 327680 | tf_op jit(solution)/shard_map/all_to_all | solution.py:70
  86.9 1.0 adjoint_in.1
  87.9 11.6 %all_to_all.61.both_ref = bf16[16,72,128]{2,1,0:T(8,128)(2,1)S(1)} all-to-all(bf16[16,72,128]{2,1,0:T(8,128)(2,1)S(1)} %adjoint_in.1), channel_id=1, replica_groups=mesh['dap'=16,'dp'=2] {'dap'}, dimensions={0} | all-to-all | bytes 589824 | tf_op jit(solution)/shard_map/all_to_all | solution.py:70
  99.5 2.0 %between.1 = (bf16[16,96,128]{2,1,0:T(8,128)(2,1)S(1)}, f32[128,640]{1,0:T(8,128)S(1)}, bf16[128,640]{1,0:T(8,128)(2,1)S(1)}) custom-call(bf16[16,72,128]{2,1,0:T(8,128)(2,1)S(1)} %all_to_all.61.both_ref, bf16[128,640]{1,0:T(8,128)(2,1)S(1)} %get-tuple-element.54.pair_ref.pair_in_ref, bf16[128,640]{1,0:T(8,128)(2,1)S(1)} %get-tuple-element.57.seed_ref, ...), custom_call_target="tpu_custom_call" | custom-call | flops 200000000 | bytes 2621440 | tf_op jit(solution)/shard_map/between/pallas_call | solution.py:418
  101.5 0.0 copy-start.1
  101.5 13.3 %all_to_all.62.grad_ref = bf16[16,96,128]{2,1,0:T(8,128)(2,1)S(1)} all-to-all(bf16[16,96,128]{2,1,0:T(8,128)(2,1)S(1)} %get-tuple-element.60), channel_id=1, replica_groups=mesh['dap'=16,'dp'=2] {'dap'}, dimensions={0} | all-to-all | bytes 786432 | tf_op jit(solution)/shard_map/all_to_all | solution.py:70
  114.8 1.0 adjoint_out.1
  115.8 15.0 %all_to_all.63.both_ref = bf16[16,128,128]{2,1,0:T(8,128)(2,1)S(1)} all-to-all(bf16[16,128,128]{2,1,0:T(8,128)(2,1)S(1)} %adjoint_out.1), channel_id=1, replica_groups=mesh['dap'=16,'dp'=2] {'dap'}, dimensions={0} | all-to-all | bytes 1048576 | tf_op jit(solution)/shard_map/all_to_all | solution.py:70
  130.8 3.8 %close.1 = (bf16[16,208,128]{2,1,0:T(8,128)(2,1)S(1)}, bf16[576,128]{1,0:T(8,128)(2,1)S(1)}, bf16[192,128]{1,0:T(8,128)(2,1)S(1)}) custom-call(bf16[16,128,128]{2,1,0:T(8,128)(2,1)S(1)} %all_to_all.63.both_ref, bf16[128,640]{1,0:T(8,128)(2,1)S(1)} %get-tuple-element.50.pair_ref.pair_out_ref, f32[128,640]{1,0:T(8,128)S(1)} %get-tuple-element.61.grad_ref, ...), custom_call_target="tpu_custom_call" | custom-call | flops 200000000 | bytes 5210112 | tf_op jit(solution)/shard_map/close/pallas_call | solution.py:418
  134.7 24.1 %all_to_all.64.parts_ref = bf16[16,208,128]{2,1,0:T(8,128)(2,1)S(1)} all-to-all(bf16[16,208,128]{2,1,0:T(8,128)(2,1)S(1)} %get-tuple-element.67), channel_id=1, replica_groups=mesh['dap'=16,'dp'=2] {'dap'}, dimensions={0} | all-to-all | bytes 1703936 | tf_op jit(solution)/shard_map/all_to_all | solution.py:70
  158.8 1.4 msa_adjoint.1
  160.2 18.3 %all_to_all.65.parts_ref = bf16[16,176,128]{2,1,0:T(8,128)(2,1)S(1)} all-to-all(bf16[16,176,128]{2,1,0:T(8,128)(2,1)S(1)} %get-tuple-element.69), channel_id=1, replica_groups=mesh['dap'=16,'dp'=2] {'dap'}, dimensions={0} | all-to-all | bytes 1441792 | tf_op jit(solution)/shard_map/all_to_all | solution.py:70
  178.5 1.5 totals.1
  (15 shorter events, 0.0 us)
Async XLA Ops:
  0.6 22.8 %copy-start.3 = (bf16[6,96,128]{2,1,0:T(8,128)(2,1)S(1)}, bf16[6,96,128]{2,1,0:T(8,128)(2,1)}, u32[]{:S(2)}) copy-start(bf16[6,96,128]{2,1,0:T(8,128)(2,1)} %param.9) | copy-start | bytes 442372
  38.5 36.5 %copy-start.6 = (bf16[128,128]{1,0:T(8,128)(2,1)S(1)}, bf16[128,128]{1,0:T(8,128)(2,1)}, u32[]{:S(2)}) copy-start(bf16[128,128]{1,0:T(8,128)(2,1)} %final_ref.1) | copy-start | bytes 98308
  38.5 36.5 %copy-start.7 = (bf16[6,96,128]{2,1,0:T(8,128)(2,1)S(1)}, bf16[6,96,128]{2,1,0:T(8,128)(2,1)}, u32[]{:S(2)}) copy-start(bf16[6,96,128]{2,1,0:T(8,128)(2,1)} %param.17) | copy-start | bytes 442372
  63.0 36.4 %copy-start.2 = (bf16[128,640]{1,0:T(8,128)(2,1)S(1)}, bf16[128,640]{1,0:T(8,128)(2,1)}, u32[]{:S(2)}) copy-start(bf16[128,640]{1,0:T(8,128)(2,1)} %gates_in_ref.1) | copy-start | bytes 491524
  63.0 36.4 %copy-start.4 = (bf16[128,128]{1,0:T(8,128)(2,1)S(1)}, bf16[128,128]{1,0:T(8,128)(2,1)}, u32[]{:S(2)}) copy-start(bf16[128,128]{1,0:T(8,128)(2,1)} %final_out_ref.1) | copy-start | bytes 98308
  101.5 29.4 %copy-start.1 = (bf16[128,640]{1,0:T(8,128)(2,1)S(1)}, bf16[128,640]{1,0:T(8,128)(2,1)}, u32[]{:S(2)}) copy-start(bf16[128,640]{1,0:T(8,128)(2,1)} %gates_ref.1) | copy-start | bytes 491524
  134.7 24.1 %copy-start = (bf16[64,6,256]{2,0,1:T(8,128)(2,1)S(1)}, bf16[64,6,256]{2,0,1:T(8,128)(2,1)}, u32[]{:S(2)}) copy-start(bf16[64,6,256]{2,0,1:T(8,128)(2,1)} %param.10) | copy-start | bytes 589828
  134.7 24.1 %copy-start.5 = (bf16[256,64]{0,1:T(8,128)(2,1)S(1)}, bf16[256,64]{0,1:T(8,128)(2,1)}, u32[]{:S(2)}) copy-start(bf16[256,64]{0,1:T(8,128)(2,1)} %param.11) | copy-start | bytes 98308
